TPU v7x, 128 devices: a whole 4x4x4 slice. The times are simulated.
128 devices in a mesh: section: 4 (over y_lo, core), expert: 32 (over x, y_hi, z).
Axes of the slice: x: 4, y: 4 (y_hi: 2, y_lo: 2; y = y_hi * 2 + y_lo), z: 4, core: 2. Of those that a mesh axis runs over, the one named last changes fastest.
Arguments:
- pending_inputs: bfloat16 [4, 1024, 4096], P('section', 'expert'), may hold values from -6 to 6
- arriving_microgroups: bfloat16 [1, 1024, 4096], P(None, 'expert'), may hold values from -6 to 6
- expert_assignment: int32 [4, 2, 1024, 2], P('section', None, 'expert'), may hold values from 0 to 3, all different within a row; in each aligned block of 32 rows (0 to 31, 32 to 63, ..., all dimensions but the last counted through in order) at most 24 rows name the same one
- segment_rescale_factor: float32 [4, 4096], P('section'), may hold values from 0.5 to 1.5
- assignment_logit_maps: float32 [4, 4096, 4], P('section'), may hold values from -0.09375 to 0.09375
- gating_projections: bfloat16 [4, 4096, 28672], P('section', None, 'expert'), may hold values from -0.09375 to 0.09375
- expanding_projections: bfloat16 [4, 4096, 28672], P('section', None, 'expert'), may hold values from -0.09375 to 0.09375
- contracting_projections: bfloat16 [4, 28672, 4096], P('section', 'expert'), may hold values from -0.0625 to 0.0625
Outputs:
- carried: bfloat16 [2, 4, 1024, 4096], P(None, 'section', 'expert')
Inputs may be any that keep to these rules, and one draw needn't show every extreme that they name: `expert_assignment`: the two experts of a row differ. Among the rows of one device (one section, one step, 32 tokens), no expert is named more than 24 times, and in every draw some expert is named exactly 24 times.
All inputs are finite; a program needn't handle non-finite values.
Results may differ from a plain program's by a relative error of at most 0.0085.
Values may be sent and summed in bfloat16 or wider, within the bound.
A program may use at most 128 MiB of HBM per device.

v0:
```python
import jax
import jax.numpy as jnp
from jax import lax
from jax.sharding import PartitionSpec as P

EXPERTS = 4
STEPS = 2
CAP = 24


epsilon = 1e-05


def shifted(x, axis, by):
    size = lax.axis_size(axis)
    return lax.ppermute(x, axis, [(i, (i + by) % size) for i in range(size)])


def expert_rows(token_rows, gate_cols, up_cols, down_rows):
    matrix = token_rows.reshape(-1, token_rows.shape[-1])
    gate_value = jnp.dot(matrix, gate_cols, preferred_element_type=jnp.float32)
    up_value = jnp.dot(matrix, up_cols, preferred_element_type=jnp.float32)
    hidden = (jax.nn.silu(gate_value) * up_value).astype(jnp.bfloat16)
    output = jnp.dot(hidden, down_rows, preferred_element_type=jnp.float32)
    return output.reshape(token_rows.shape[0], token_rows.shape[1], -1)


def route_slots(chosen):
    chosen_flat = chosen.reshape(-1)
    expert_hits = (chosen_flat[:, None] == jnp.arange(EXPERTS, dtype=jnp.int32)[None, :]).astype(
        jnp.int32
    )
    before = jnp.cumsum(expert_hits, 0) - expert_hits
    position = jnp.sum(before * expert_hits, 1)
    return chosen_flat * CAP + position


def moe_layer(
    activation,
    chosen,
    segment_rescale_factor,
    assignment_logit_maps,
    gate_cols,
    up_cols,
    down_rows,
    group_size,
):
    as_float = activation.astype(jnp.float32)
    normed = (
        as_float
        * lax.rsqrt(jnp.mean(as_float * as_float, -1, keepdims=True) + epsilon)
        * segment_rescale_factor
    ).astype(jnp.bfloat16)
    logits = jnp.dot(
        normed.astype(jnp.float32), assignment_logit_maps, precision=lax.Precision.HIGHEST
    )
    chooses = chosen[:, :, None] == jnp.arange(EXPERTS, dtype=jnp.int32)[None, None, :]
    picked = jnp.sum(jnp.where(chooses, logits[:, None, :], 0.0), -1)
    first_share = jax.nn.sigmoid(picked[:, 0] - picked[:, 1])
    share_pair = jnp.stack([first_share, 1.0 - first_share], 1).astype(jnp.bfloat16)
    model_width = activation.shape[-1]
    slot_index = route_slots(chosen)
    places = jnp.arange(EXPERTS * CAP, dtype=jnp.int32)
    selector = (places[:, None] == slot_index[None, :]).astype(jnp.bfloat16)
    doubled = jnp.repeat(normed, 2, axis=0)
    routed = jnp.dot(selector, doubled, preferred_element_type=jnp.float32).astype(jnp.bfloat16)
    copies = jnp.broadcast_to(
        routed.reshape(EXPERTS, 1, CAP, model_width), (EXPERTS, group_size, CAP, model_width)
    )
    copies = copies.reshape(EXPERTS * group_size, CAP, model_width)
    partial_value = expert_rows(
        lax.all_to_all(copies, "expert", split_axis=0, concat_axis=0, tiled=True),
        gate_cols,
        up_cols,
        down_rows,
    )
    returned = lax.all_to_all(
        partial_value.astype(jnp.bfloat16), "expert", split_axis=0, concat_axis=0, tiled=True
    ).astype(partial_value.dtype)
    expert_out = jnp.sum(returned.reshape(EXPERTS, group_size, CAP, model_width), 1).reshape(
        EXPERTS * CAP, model_width
    )
    combiner = jnp.where(
        slot_index[:, None] == places[None, :],
        share_pair.reshape(-1).astype(jnp.float32)[:, None],
        0.0,
    )
    mixture = jnp.dot(combiner, expert_out, precision=lax.Precision.HIGHEST)
    mixture = jnp.sum(mixture.reshape(activation.shape[0], 2, model_width), 1)
    return (as_float + mixture).astype(jnp.bfloat16)


def shards(
    pending_inputs,
    arriving_microgroups,
    expert_assignment,
    segment_rescale_factor,
    assignment_logit_maps,
    gating_projections,
    expanding_projections,
    contracting_projections,
):
    section_index = lax.axis_index("section")
    group_size = lax.axis_size("expert") // EXPERTS
    present_activation = pending_inputs[0]
    records = []
    for step_index in range(STEPS):
        if step_index > 0:
            present_activation = jnp.where(
                section_index == 0, arriving_microgroups[step_index - 1], present_activation
            )
        result = moe_layer(
            present_activation,
            expert_assignment[0, step_index],
            segment_rescale_factor[0],
            assignment_logit_maps[0],
            gating_projections[0],
            expanding_projections[0],
            contracting_projections[0],
            group_size,
        )
        present_activation = shifted(result, "section", 1)
        records.append(present_activation)
    return jnp.stack(records)[:, None]


def solution(mesh):
    return jax.shard_map(
        shards,
        mesh=mesh,
        in_specs=(
            P("section", "expert", None),
            P(None, "expert", None),
            P("section", None, "expert", None),
            P("section", None),
            P("section", None, None),
            P("section", None, "expert"),
            P("section", None, "expert"),
            P("section", "expert", None),
        ),
        out_specs=P(None, "section", "expert", None),
        check_vma=False,
    )
```

profile of v0, /device:TPU:1, one launch (start us, length us, event | category | flops | bytes accessed | tf_op | source)
XLA Modules:
  0.0 422.4 jit_solution(482754948778298741)
XLA Ops:
  0.0 1.1 fusion.25
  1.2 1.3 slice_bitcast_fusion
  3.0 1.1 fusion.27
  4.1 0.5 broadcast_in_dim.81
  4.8 0.3 convolution_convert_fusion.1
  5.1 0.8 broadcast_in_dim.83
  5.9 84.0 %all_to_all.20 = bf16[32,24,4096]{2,1,0:T(8,128)(2,1)S(1)} all-to-all(bf16[32,24,4096]{2,1,0:T(8,128)(2,1)S(1)} %bitcast.103), channel_id=1, replica_groups=mesh['section'=4,'expert'=32] {'expert'}, dimensions={0} | all-to-all | bytes 12582912 | tf_op jit(solution)/shard_map/all_to_all | solution.py:72
  89.9 6.7 %fusion.6 = f32[768,896]{1,0:T(8,128)S(1)} fusion(bf16[768,4096]{1,0:T(8,128)(2,1)S(1)} %bitcast.105, bf16[1,4096,896]{2,1,0:T(8,128)(2,1)S(1)} %bitcast.119), kind=kOutput, calls=%fused_computation.8 | convolution fusion | flops 5637144576 | bytes 16384000 | tf_op jit(solution)/shard_map/dot_general | solution.py:22
  96.7 7.0 %multiply_convert_fusion.1 = bf16[768,896]{1,0:T(8,128)(2,1)S(1)} fusion(f32[768,896]{1,0:T(8,128)S(1)} %fusion.6, bf16[768,4096]{1,0:T(8,128)(2,1)S(1)} %bitcast.106, bf16[1,4096,896]{2,1,0:T(8,128)(2,1)S(1)} %bitcast.123), kind=kOutput, calls=%fused_computation.19 | convolution fusion | flops 5641273344 | bytes 17760256 | tf_op jit(solution)/shard_map/dot_general | solution.py:21
  103.7 8.6 %fusion.12 = bf16[32,24,4096]{2,1,0:T(8,128)(2,1)} fusion(bf16[32,24,896]{2,1,0:T(8,128)(2,1)S(1)} %bitcast.130, bf16[1,896,4096]{2,1,0:T(8,128)(2,1)S(1)} %bitcast.127), kind=kOutput, calls=%fused_computation.14 | convolution fusion | flops 5640290304 | bytes 15007744 | tf_op jit(solution)/shard_map/dot_general | solution.py:24
  112.3 6.5 %all-to-all-start.1 = ((bf16[32,24,4096]{2,1,0:T(8,128)(2,1)}), bf16[32,24,4096]{2,1,0:T(8,128)(2,1)}, u32[]{:S(2)}, u32[]{:S(2)}) async-start(bf16[32,24,4096]{2,1,0:T(8,128)(2,1)} %fusion.12), calls=%async_computation.1 | async-start | bytes 12582912 | tf_op jit(solution)/shard_map/all_to_all | solution.py:77
  119.8 0.4 fusion.36
  120.3 83.2 %all-to-all-done.1 = bf16[32,24,4096]{2,1,0:T(8,128)(2,1)} async-done(((bf16[32,24,4096]{2,1,0:T(8,128)(2,1)}), bf16[32,24,4096]{2,1,0:T(8,128)(2,1)}, u32[]{:S(2)}, u32[]{:S(2)}) %all-to-all-start.1) | async-done | bytes 6291488 | tf_op jit(solution)/shard_map/all_to_all | solution.py:77
  203.4 4.0 convert_reduce_fusion.1
  207.5 1.2 convolution_reduce_fusion.1
  208.8 0.4 collective-permute-start
  209.2 3.3 collective-permute-done
  212.5 0.2 fusion.31
  212.8 0.5 broadcast_in_dim.86
  213.5 0.3 convolution_convert_fusion
  213.9 0.8 broadcast_in_dim.88
  214.7 81.5 %all_to_all.21 = bf16[32,24,4096]{2,1,0:T(8,128)(2,1)S(1)} all-to-all(bf16[32,24,4096]{2,1,0:T(8,128)(2,1)S(1)} %bitcast.104), channel_id=1, replica_groups=mesh['section'=4,'expert'=32] {'expert'}, dimensions={0} | all-to-all | bytes 12582912 | tf_op jit(solution)/shard_map/all_to_all | solution.py:72
  296.2 6.7 %fusion.4 = f32[768,896]{1,0:T(8,128)S(1)} fusion(bf16[768,4096]{1,0:T(8,128)(2,1)S(1)} %bitcast.107, bf16[1,4096,896]{2,1,0:T(8,128)(2,1)S(1)} %bitcast.121), kind=kOutput, calls=%fused_computation.6 | convolution fusion | flops 5637144576 | bytes 16384000 | tf_op jit(solution)/shard_map/dot_general | solution.py:22
  303.0 7.0 %multiply_convert_fusion = bf16[768,896]{1,0:T(8,128)(2,1)S(1)} fusion(f32[768,896]{1,0:T(8,128)S(1)} %fusion.4, bf16[768,4096]{1,0:T(8,128)(2,1)S(1)} %bitcast.108, bf16[1,4096,896]{2,1,0:T(8,128)(2,1)S(1)} %bitcast.125), kind=kOutput, calls=%fused_computation.18 | convolution fusion | flops 5641273344 | bytes 17760256 | tf_op jit(solution)/shard_map/dot_general | solution.py:21
  310.0 8.6 %fusion.15 = bf16[32,24,4096]{2,1,0:T(8,128)(2,1)} fusion(bf16[32,24,896]{2,1,0:T(8,128)(2,1)S(1)} %bitcast.131, bf16[1,896,4096]{2,1,0:T(8,128)(2,1)S(1)} %bitcast.129), kind=kOutput, calls=%fused_computation.15 | convolution fusion | flops 5640290304 | bytes 15007744 | tf_op jit(solution)/shard_map/dot_general | solution.py:24
  318.6 10.4 %all-to-all-start.3 = ((bf16[32,24,4096]{2,1,0:T(8,128)(2,1)}), bf16[32,24,4096]{2,1,0:T(8,128)(2,1)}, u32[]{:S(2)}, u32[]{:S(2)}) async-start(bf16[32,24,4096]{2,1,0:T(8,128)(2,1)} %fusion.15), calls=%async_computation.3 | async-start | bytes 12582912 | tf_op jit(solution)/shard_map/all_to_all | solution.py:77
  329.0 0.3 fusion.40
  329.4 83.5 %all-to-all-done.3 = bf16[32,24,4096]{2,1,0:T(8,128)(2,1)} async-done(((bf16[32,24,4096]{2,1,0:T(8,128)(2,1)}), bf16[32,24,4096]{2,1,0:T(8,128)(2,1)}, u32[]{:S(2)}, u32[]{:S(2)}) %all-to-all-start.3) | async-done | bytes 6291488 | tf_op jit(solution)/shard_map/all_to_all | solution.py:77
  412.9 4.0 convert_reduce_fusion
  416.9 1.2 convolution_reduce_fusion
  418.3 3.3 collective-permute-done.1
  421.6 0.8 maximum_bitcast_fusion
  (75 shorter events, 2.4 us)
Async XLA Ops:
  0.0 119.7 %copy-start = (f32[1,4096,4]{1,2,0:T(4,128)S(1)}, f32[1,4096,4]{1,2,0:T(4,128)}, u32[]{:S(2)}) copy-start(f32[1,4096,4]{1,2,0:T(4,128)} %param.12) | copy-start | bytes 196612
  5.1 84.8 %slice-start = ((s8[7340032]{0:T(1024)(128)(4,1)}), s8[3145728]{0:T(1024)(128)(4,1)S(1)}, s32[]{:S(2)}) async-start(s8[7340032]{0:T(1024)(128)(4,1)} %bitcast.118), calls=%async_computation.4 | async-start | bytes 6291456
  5.9 84.0 %slice-start.1 = ((s8[7340032]{0:T(1024)(128)(4,1)}), s8[4194304]{0:T(1024)(128)(4,1)S(1)}, s32[]{:S(2)}) async-start(s8[7340032]{0:T(1024)(128)(4,1)} %bitcast.118), calls=%async_computation.5 | async-start | bytes 8388608
  5.9 90.7 %slice-start.4 = ((s8[7340032]{0:T(1024)(128)(4,1)}), s8[4194304]{0:T(1024)(128)(4,1)S(1)}, s32[]{:S(2)}) async-start(s8[7340032]{0:T(1024)(128)(4,1)} %bitcast.122), calls=%async_computation.8 | async-start | bytes 8388608
  89.9 6.7 %slice-start.5 = ((s8[7340032]{0:T(1024)(128)(4,1)}), s8[3145728]{0:T(1024)(128)(4,1)S(1)}, s32[]{:S(2)}) async-start(s8[7340032]{0:T(1024)(128)(4,1)} %bitcast.122), calls=%async_computation.9 | async-start | bytes 6291456
  89.9 13.7 %slice-start.8 = ((s8[7340032]{0:T(1024)(128)(4,1)}), s8[4194304]{0:T(1024)(128)(4,1)S(1)}, s32[]{:S(2)}) async-start(s8[7340032]{0:T(1024)(128)(4,1)} %bitcast.126), calls=%async_computation.12 | async-start | bytes 8388608
  96.7 7.0 %slice-start.9 = ((s8[7340032]{0:T(1024)(128)(4,1)}), s8[3145728]{0:T(1024)(128)(4,1)S(1)}, s32[]{:S(2)}) async-start(s8[7340032]{0:T(1024)(128)(4,1)} %bitcast.126), calls=%async_computation.13 | async-start | bytes 6291456
  112.3 7.5 %copy-start.1 = (bf16[1,32,4096]{2,1,0:T(8,128)(2,1)S(1)}, bf16[1,32,4096]{2,1,0:T(8,128)(2,1)}, u32[]{:S(2)}) copy-start(bf16[1,32,4096]{2,1,0:T(8,128)(2,1)} %param.8) | copy-start | bytes 786436
  112.3 7.5 %copy-start.3 = (f32[1,4096]{1,0:T(1,128)S(1)}, f32[1,4096]{1,0:T(1,128)}, u32[]{:S(2)}) copy-start(f32[1,4096]{1,0:T(1,128)} %param.11) | copy-start | bytes 49156
  112.3 8.0 %copy-start.4 = (s32[1,2,32,2]{2,3,1,0:T(2,128)S(1)}, s32[1,2,32,2]{2,3,1,0:T(2,128)}, u32[]{:S(2)}) copy-start(s32[1,2,32,2]{2,3,1,0:T(2,128)} %param.10) | copy-start | bytes 1540
  112.3 91.2 %all-to-all-start.1 = ((bf16[32,24,4096]{2,1,0:T(8,128)(2,1)}), bf16[32,24,4096]{2,1,0:T(8,128)(2,1)}, u32[]{:S(2)}, u32[]{:S(2)}) async-start(bf16[32,24,4096]{2,1,0:T(8,128)(2,1)} %fusion.12), calls=%async_computation.1 | async-start | bytes 12582912 | tf_op jit(solution)/shard_map/all_to_all | solution.py:77
  118.8 93.7 %copy-start.2 = (bf16[1,32,4096]{2,1,0:T(8,128)(2,1)S(1)}, bf16[1,32,4096]{2,1,0:T(8,128)(2,1)}, u32[]{:S(2)}) copy-start(bf16[1,32,4096]{2,1,0:T(8,128)(2,1)} %param.9) | copy-start | bytes 786436
  208.8 3.7 collective-permute-start
  213.9 82.3 %slice-start.2 = ((s8[7340032]{0:T(1024)(128)(4,1)}), s8[3145728]{0:T(1024)(128)(4,1)S(1)}, s32[]{:S(2)}) async-start(s8[7340032]{0:T(1024)(128)(4,1)} %bitcast.120), calls=%async_computation.6 | async-start | bytes 6291456
  214.7 81.5 %slice-start.3 = ((s8[7340032]{0:T(1024)(128)(4,1)}), s8[4194304]{0:T(1024)(128)(4,1)S(1)}, s32[]{:S(2)}) async-start(s8[7340032]{0:T(1024)(128)(4,1)} %bitcast.120), calls=%async_computation.7 | async-start | bytes 8388608
  214.7 88.2 %slice-start.6 = ((s8[7340032]{0:T(1024)(128)(4,1)}), s8[4194304]{0:T(1024)(128)(4,1)S(1)}, s32[]{:S(2)}) async-start(s8[7340032]{0:T(1024)(128)(4,1)} %bitcast.124), calls=%async_computation.10 | async-start | bytes 8388608
  296.2 6.7 %slice-start.7 = ((s8[7340032]{0:T(1024)(128)(4,1)}), s8[3145728]{0:T(1024)(128)(4,1)S(1)}, s32[]{:S(2)}) async-start(s8[7340032]{0:T(1024)(128)(4,1)} %bitcast.124), calls=%async_computation.11 | async-start | bytes 6291456
  296.2 13.7 %slice-start.10 = ((s8[7340032]{0:T(1024)(128)(4,1)}), s8[4194304]{0:T(1024)(128)(4,1)S(1)}, s32[]{:S(2)}) async-start(s8[7340032]{0:T(1024)(128)(4,1)} %bitcast.128), calls=%async_computation.14 | async-start | bytes 8388608
  302.9 7.0 %slice-start.11 = ((s8[7340032]{0:T(1024)(128)(4,1)}), s8[3145728]{0:T(1024)(128)(4,1)S(1)}, s32[]{:S(2)}) async-start(s8[7340032]{0:T(1024)(128)(4,1)} %bitcast.128), calls=%async_computation.15 | async-start | bytes 6291456
  318.5 10.7 %copy-start.5 = (s32[32,2]{0,1:T(2,128)S(1)}, s32[32,2]{0,1:T(2,128)}, u32[]{:S(2)}) copy-start(s32[32,2]{0,1:T(2,128)} %get-tuple-element.13) | copy-start | bytes 772
  318.6 94.3 %all-to-all-start.3 = ((bf16[32,24,4096]{2,1,0:T(8,128)(2,1)}), bf16[32,24,4096]{2,1,0:T(8,128)(2,1)}, u32[]{:S(2)}, u32[]{:S(2)}) async-start(bf16[32,24,4096]{2,1,0:T(8,128)(2,1)} %fusion.15), calls=%async_computation.3 | async-start | bytes 12582912 | tf_op jit(solution)/shard_map/all_to_all | solution.py:77
  418.2 3.4 collective-permute-start.1
where the time goes:
time: 431 us; the launch traced here: 422 us
  waiting for transfers between devices  173 us (40%)
  blocking collectives  165 us (38%)
  matrix products  48.3 us (11%)
  starting transfers between devices  17.4 us (4%)
  other arithmetic  12.5 us (3%)
  local copies, waits for them, and re-layouts  4.99 us (1%)
    all_to_all x2, waiting for transfers between devices, moe_layer(): lax.all_to_all(partial_value.astype(jnp.bfloat16), 'expert', split_axis=0...  167 us
    all_to_all x2, blocking collectives, moe_layer(): lax.all_to_all(copies, 'expert', split_axis=0, concat_axis=0, tiled=True)  165 us
    dot_general x2, matrix products, expert_rows(): output = jnp.dot(hidden, down_rows, preferred_element_type=jnp.float32)  17.1 us
    all_to_all x2, starting transfers between devices, moe_layer(): lax.all_to_all(partial_value.astype(jnp.bfloat16), 'expert', split_axis=0...  16.9 us
    dot_general x2, matrix products, expert_rows(): gate_value = jnp.dot(matrix, gate_cols, preferred_element_type=jnp.float32)  14 us
    dot_general x2, matrix products, expert_rows(): up_value = jnp.dot(matrix, up_cols, preferred_element_type=jnp.float32)  13.4 us
  transfers between devices with their start and end apart: 4, of which 4 were waited for; matrix products, arithmetic and copies ran while one was open for 0% of the time, Pallas kernels for 0%

commit v1 on v0

v1 whole, which is shorter than its diff:
```python
import jax
import jax.numpy as jnp
from jax import lax
from jax.sharding import PartitionSpec as P

EXPERTS = 4
STEPS = 2

epsilon = 1e-05


def shifted(x, axis, by):
    size = lax.axis_size(axis)
    return lax.ppermute(x, axis, [(i, (i + by) % size) for i in range(size)])


def moe_layer(activation, chosen, gain, router, gate_cols, up_cols, down_rows, group_size):
    as_float = activation.astype(jnp.float32)
    normed = (
        as_float
        * lax.rsqrt(jnp.mean(as_float * as_float, -1, keepdims=True) + epsilon)
        * gain
    ).astype(jnp.bfloat16)
    logits = jnp.dot(normed.astype(jnp.float32), router, precision=lax.Precision.HIGHEST)
    chooses = chosen[:, :, None] == jnp.arange(EXPERTS, dtype=jnp.int32)[None, None, :]
    picked = jnp.sum(jnp.where(chooses, logits[:, None, :], 0.0), -1)
    first_share = jax.nn.sigmoid(picked[:, 0] - picked[:, 1])
    share_pair = jnp.stack([first_share, 1.0 - first_share], 1).astype(jnp.bfloat16)
    weights = jnp.sum(jnp.where(chooses, share_pair[:, :, None].astype(jnp.float32), 0.0), 1)
    width = activation.shape[-1]
    extra = jnp.pad(weights.astype(jnp.bfloat16), ((0, 0), (0, 128 - EXPERTS)))
    packed = jnp.concatenate([normed, extra], 1)
    every = lax.all_gather(packed, "expert", axis=0, tiled=True)
    rows = every[:, :width]
    mine = lax.axis_index("expert") // group_size
    lanes = jnp.arange(128, dtype=jnp.int32)[None, :] == mine
    weight = jnp.sum(jnp.where(lanes, every[:, width:].astype(jnp.float32), 0.0), 1)
    gate_value = jnp.dot(rows, gate_cols, preferred_element_type=jnp.float32)
    up_value = jnp.dot(rows, up_cols, preferred_element_type=jnp.float32)
    hidden = (jax.nn.silu(gate_value) * up_value).astype(jnp.bfloat16)
    output = jnp.dot(hidden, down_rows, preferred_element_type=jnp.float32) * weight[:, None]
    mixture = lax.psum_scatter(
        output.astype(jnp.bfloat16), "expert", scatter_dimension=0, tiled=True
    )
    return (as_float + mixture.astype(jnp.float32)).astype(jnp.bfloat16)


def shards(
    pending_inputs,
    arriving_microgroups,
    expert_assignment,
    segment_rescale_factor,
    assignment_logit_maps,
    gating_projections,
    expanding_projections,
    contracting_projections,
):
    section_index = lax.axis_index("section")
    group_size = lax.axis_size("expert") // EXPERTS
    present_activation = pending_inputs[0]
    records = []
    for step_index in range(STEPS):
        if step_index > 0:
            present_activation = jnp.where(
                section_index == 0, arriving_microgroups[step_index - 1], present_activation
            )
        result = moe_layer(
            present_activation,
            expert_assignment[0, step_index],
            segment_rescale_factor[0],
            assignment_logit_maps[0],
            gating_projections[0],
            expanding_projections[0],
            contracting_projections[0],
            group_size,
        )
        present_activation = shifted(result, "section", 1)
        records.append(present_activation)
    return jnp.stack(records)[:, None]


def solution(mesh):
    return jax.shard_map(
        shards,
        mesh=mesh,
        in_specs=(
            P("section", "expert", None),
            P(None, "expert", None),
            P("section", None, "expert", None),
            P("section", None),
            P("section", None, None),
            P("section", None, "expert"),
            P("section", None, "expert"),
            P("section", "expert", None),
        ),
        out_specs=P(None, "section", "expert", None),
        check_vma=False,
    )
```

time: 431 us -> 721 us (1.67); the launches traced: 422 us -> 720 us
  waiting for transfers between devices: 173 us -> 574 us
  blocking collectives: 165 us -> 0 us
  starting transfers between devices: 17.4 us -> 50.9 us
  matrix products: 48.3 us -> 72.8 us
  between operations: 0.48 us -> 13.4 us
    reduce_scatter x0 -> x2, waiting for transfers between devices: none -> 358 us  [moe_layer(): lax.psum_scatter(output.astype(jnp.bfloat16), 'expert', scatter_dimension...]
    all_gather x0 -> x2, waiting for transfers between devices: none -> 209 us  [moe_layer(): every = lax.all_gather(packed, 'expert', axis=0, tiled=True)]
    all_to_all x2 -> x0, waiting for transfers between devices: 167 us -> none  [moe_layer(): lax.all_to_all(partial_value.astype(jnp.bfloat16), 'expert', split_axis=0...]
    all_to_all x2 -> x0, blocking collectives: 165 us -> none  [moe_layer(): lax.all_to_all(copies, 'expert', split_axis=0, concat_axis=0, tiled=True)]
    ppermute x2, starting transfers between devices: 0.47 us -> 50.6 us  [shifted(): return lax.ppermute(x, axis, [(i, (i + by) % size) for i in range(size)])]
    dot_general x12 -> x8, matrix products: 48.3 us -> 72.8 us  [the longest x2 25 us: moe_layer(): up_value = jnp.dot(rows, up_cols, preferred_element_type=jnp.float32)]
    all_to_all x2 -> x0, starting transfers between devices: 16.9 us -> none  [moe_layer(): lax.all_to_all(partial_value.astype(jnp.bfloat16), 'expert', split_axis=0...]
  transfers between devices with their start and end apart: 4 -> 6, of which waited for: 4 -> 6; matrix products, arithmetic and copies ran while one was open for 0% -> 0% of each run, Pallas kernels for 0% -> 0%
where the time goes in v1:
time: 721 us; the launch traced here: 720 us
  waiting for transfers between devices  574 us (80%)
  matrix products  72.8 us (10%)
  starting transfers between devices  50.9 us (7%)
  between operations  13.4 us (2%)
  other arithmetic  8.33 us (1%)
    reduce_scatter x2, waiting for transfers between devices, moe_layer(): lax.psum_scatter(output.astype(jnp.bfloat16), 'expert', scatter_dimension...  358 us
    all_gather x2, waiting for transfers between devices, moe_layer(): every = lax.all_gather(packed, 'expert', axis=0, tiled=True)  209 us
    ppermute x2, starting transfers between devices, shifted(): return lax.ppermute(x, axis, [(i, (i + by) % size) for i in range(size)])  50.6 us
    dot_general x2, matrix products, moe_layer(): up_value = jnp.dot(rows, up_cols, preferred_element_type=jnp.float32)  25 us
    dot_general x2, matrix products, moe_layer(): gate_value = jnp.dot(rows, gate_cols, preferred_element_type=jnp.float32)  24 us
    dot_general x2, matrix products, moe_layer(): jnp.dot(hidden, down_rows, preferred_element_type=jnp.float32)  22.1 us
  transfers between devices with their start and end apart: 6, of which 6 were waited for; matrix products, arithmetic and copies ran while one was open for 0% of the time, Pallas kernels for 0%

profile of v1, /device:TPU:1, one launch (start us, length us, event | category | flops | bytes accessed | tf_op | source)
XLA Modules:
  0.0 720.5 jit_solution(6678355613342808113)
XLA Ops:
  6.5 1.1 fusion.27
  7.7 1.1 fusion.29
  8.8 1.3 fusion.40
  10.1 0.7 slice_bitcast_fusion
  10.9 0.1 copy.27
  11.0 0.7 fusion.37
  11.8 0.0 reduce-scatter.3.cloned.1.call-start
  11.9 107.8 %all-gather.3.cloned.1.call-done = bf16[1024,4224]{1,0:T(8,128)(2,1)} async-done(((bf16[32,4224]{1,0:T(8,128)(2,1)}), bf16[1024,4224]{1,0:T(8,128)(2,1)}) %all-gather.3.cloned.1.call-update) | async-done | bytes 8650768 | tf_op jit(solution)/shard_map/all_gather | solution.py:33
  119.7 1.1 select_reduce_fusion.1
  120.8 12.5 %fusion.4 = f32[1024,896]{1,0:T(8,128)S(1)} fusion(bf16[1024,4224]{1,0:T(8,128)(2,1)} %all-gather.3.cloned.1.call-done, bf16[1,4096,896]{2,1,0:T(8,128)(2,1)} %param.14), kind=kOutput, calls=%fused_computation.6 | convolution fusion | flops 7516192768 | bytes 19398656 | tf_op jit(solution)/shard_map/dot_general | solution.py:39
  133.3 12.0 %multiply_convert_fusion.3 = bf16[1024,896]{1,0:T(8,128)(2,1)S(1)} fusion(f32[1024,896]{1,0:T(8,128)S(1)} %fusion.4, bf16[1,4096,896]{2,1,0:T(8,128)(2,1)} %param.13, bf16[1024,4224]{1,0:T(8,128)(2,1)S(1)} %copy-done.5), kind=kOutput, calls=%fused_computation.17 | convolution fusion | flops 7521697792 | bytes 21233664 | tf_op jit(solution)/shard_map/dot_general | solution.py:38
  145.4 11.1 %multiply_convert_fusion.1 = bf16[1024,4096]{1,0:T(8,128)(2,1)} fusion(bf16[1024,896]{1,0:T(8,128)(2,1)S(1)} %multiply_convert_fusion.3, f32[1024]{0:T(1024)S(1)} %select_reduce_fusion.1, bf16[1,896,4096]{2,1,0:T(8,128)(2,1)S(1)} %bitcast.66), kind=kOutput, calls=%fused_computation.1 | convolution fusion | flops 7524581376 | bytes 17567744 | tf_op jit(solution)/shard_map/dot_general | solution.py:41
  156.5 178.8 %reduce-scatter.3.cloned.1.call-done = bf16[32,4096]{1,0:T(8,128)(2,1)} async-done(((bf16[1024,4096]{1,0:T(8,128)(2,1)}), bf16[32,4096]{1,0:T(8,128)(2,1)}) %reduce-scatter.3.cloned.1.call-update) | async-done | bytes 262160 | tf_op jit(solution)/shard_map/reduce_scatter | solution.py:42
  335.4 1.0 fusion.30
  336.4 25.4 %collective-permute-start = (bf16[32,4096]{1,0:T(8,128)(2,1)S(1)}, bf16[32,4096]{1,0:T(8,128)(2,1)S(1)}, u32[]{:S(2)}, u32[]{:S(2)}) collective-permute-start(bf16[32,4096]{1,0:T(8,128)(2,1)S(1)} %fusion.30), channel_id=1, source_target_pairs={{0,32},{32,64},{64,96},{96,0},{1,33},{33,65},{65,97},{97,1},{2,34}... | collective-permute-start | bytes 786440 | tf_op jit(solution)/shard_map/ppermute | solution.py:14
  361.8 3.3 collective-permute-done
  365.1 0.2 fusion.33
  365.4 0.1 fusion.35
  365.5 0.3 fusion.44
  365.9 0.1 copy.28
  366.0 0.7 fusion.38
  366.8 0.2 reduce-scatter.5.cloned.1.call-start
  367.0 101.3 %all-gather.5.cloned.1.call-done = bf16[1024,4224]{1,0:T(8,128)(2,1)} async-done(((bf16[32,4224]{1,0:T(8,128)(2,1)}), bf16[1024,4224]{1,0:T(8,128)(2,1)}) %all-gather.5.cloned.1.call-update) | async-done | bytes 8650768 | tf_op jit(solution)/shard_map/all_gather | solution.py:33
  468.3 12.5 %fusion = f32[1024,896]{1,0:T(8,128)S(1)} fusion(bf16[1024,4224]{1,0:T(8,128)(2,1)} %all-gather.5.cloned.1.call-done, bf16[1,4096,896]{2,1,0:T(8,128)(2,1)} %param.14), kind=kOutput, calls=%fused_computation.2 | convolution fusion | flops 7516192768 | bytes 19398656 | tf_op jit(solution)/shard_map/dot_general | solution.py:39
  480.8 0.1 select_reduce_fusion
  481.0 12.0 %multiply_convert_fusion.2 = bf16[1024,896]{1,0:T(8,128)(2,1)S(1)} fusion(f32[1024,896]{1,0:T(8,128)S(1)} %fusion, bf16[1,4096,896]{2,1,0:T(8,128)(2,1)} %param.13, bf16[1024,4224]{1,0:T(8,128)(2,1)S(1)} %copy-done.6), kind=kOutput, calls=%fused_computation.16 | convolution fusion | flops 7521697792 | bytes 21233664 | tf_op jit(solution)/shard_map/dot_general | solution.py:38
  493.0 11.1 %multiply_convert_fusion = bf16[1024,4096]{1,0:T(8,128)(2,1)} fusion(bf16[1024,896]{1,0:T(8,128)(2,1)S(1)} %multiply_convert_fusion.2, f32[1024]{0:T(1024)S(1)} %select_reduce_fusion, bf16[1,896,4096]{2,1,0:T(8,128)(2,1)S(1)} %bitcast.68), kind=kOutput, calls=%fused_computation | convolution fusion | flops 7524581376 | bytes 17567744 | tf_op jit(solution)/shard_map/dot_general | solution.py:41
  504.1 179.4 %reduce-scatter.5.cloned.1.call-done = bf16[32,4096]{1,0:T(8,128)(2,1)} async-done(((bf16[1024,4096]{1,0:T(8,128)(2,1)}), bf16[32,4096]{1,0:T(8,128)(2,1)}) %reduce-scatter.5.cloned.1.call-update) | async-done | bytes 262160 | tf_op jit(solution)/shard_map/reduce_scatter | solution.py:42
  683.5 1.0 fusion.36
  684.6 25.2 %collective-permute-start.1 = (bf16[32,4096]{1,0:T(8,128)(2,1)S(1)}, bf16[32,4096]{1,0:T(8,128)(2,1)S(1)}, u32[]{:S(2)}, u32[]{:S(2)}) collective-permute-start(bf16[32,4096]{1,0:T(8,128)(2,1)S(1)} %fusion.36), channel_id=1, source_target_pairs={{0,32},{32,64},{64,96},{96,0},{1,33},{33,65},{65,97},{97,1},{2,34}... | collective-permute-start | bytes 786440 | tf_op jit(solution)/shard_map/ppermute | solution.py:14
  709.8 3.3 collective-permute-done.1
  713.1 0.8 maximum_bitcast_fusion
  (43 shorter events, 0.3 us)
Async XLA Ops:
  6.5 2.2 copy-start
  6.5 113.2 %all-gather.3.cloned.1.call-start = ((), (), s32[]{:S(2)}) async-start(), calls=%async_computation.2 | async-start | bytes 8921088 | tf_op jit(solution)/shard_map/all_gather | solution.py:33
  11.8 323.6 %reduce-scatter.3.cloned.1.call-start = ((), (), s32[]{:S(2)}) async-start(), calls=%async_computation.3 | async-start | bytes 8650752 | tf_op jit(solution)/shard_map/reduce_scatter | solution.py:42
  120.8 12.5 %copy-start.5 = (bf16[1024,4224]{1,0:T(8,128)(2,1)S(1)}, bf16[1024,4224]{1,0:T(8,128)(2,1)}, u32[]{:S(2)}) copy-start(bf16[1024,4224]{1,0:T(8,128)(2,1)} %all-gather.3.cloned.1.call-done) | copy-start | bytes 25952260
  120.8 24.6 %slice-start = ((s8[7340032]{0:T(1024)(128)(4,1)}), s8[4194304]{0:T(1024)(128)(4,1)S(1)}, s32[]{:S(2)}) async-start(s8[7340032]{0:T(1024)(128)(4,1)} %bitcast.65), calls=%async_computation.6 | async-start | bytes 8388608
  133.3 12.0 %slice-start.1 = ((s8[7340032]{0:T(1024)(128)(4,1)}), s8[3145728]{0:T(1024)(128)(4,1)S(1)}, s32[]{:S(2)}) async-start(s8[7340032]{0:T(1024)(128)(4,1)} %bitcast.65), calls=%async_computation.7 | async-start | bytes 6291456
  156.5 178.9 %copy-start.2 = (bf16[1,32,4096]{2,1,0:T(8,128)(2,1)S(1)}, bf16[1,32,4096]{2,1,0:T(8,128)(2,1)}, u32[]{:S(2)}) copy-start(bf16[1,32,4096]{2,1,0:T(8,128)(2,1)} %param.8) | copy-start | bytes 786436
  156.5 208.7 %copy-start.3 = (bf16[1,32,4096]{2,1,0:T(8,128)(2,1)S(1)}, bf16[1,32,4096]{2,1,0:T(8,128)(2,1)}, u32[]{:S(2)}) copy-start(bf16[1,32,4096]{2,1,0:T(8,128)(2,1)} %param.9) | copy-start | bytes 786436
  156.5 208.9 %copy-start.4 = (f32[1,4096]{1,0:T(1,128)S(1)}, f32[1,4096]{1,0:T(1,128)}, u32[]{:S(2)}) copy-start(f32[1,4096]{1,0:T(1,128)} %param.11) | copy-start | bytes 49156
  156.5 311.8 %all-gather.5.cloned.1.call-start = ((), (), s32[]{:S(2)}) async-start(), calls=%async_computation.4 | async-start | bytes 8921088 | tf_op jit(solution)/shard_map/all_gather | solution.py:33
  336.4 28.7 %collective-permute-start = (bf16[32,4096]{1,0:T(8,128)(2,1)S(1)}, bf16[32,4096]{1,0:T(8,128)(2,1)S(1)}, u32[]{:S(2)}, u32[]{:S(2)}) collective-permute-start(bf16[32,4096]{1,0:T(8,128)(2,1)S(1)} %fusion.30), channel_id=1, source_target_pairs={{0,32},{32,64},{64,96},{96,0},{1,33},{33,65},{65,97},{97,1},{2,34}... | collective-permute-start | bytes 786440 | tf_op jit(solution)/shard_map/ppermute | solution.py:14
  366.8 316.8 %reduce-scatter.5.cloned.1.call-start = ((), (), s32[]{:S(2)}) async-start(), calls=%async_computation.5 | async-start | bytes 8650752 | tf_op jit(solution)/shard_map/reduce_scatter | solution.py:42
  468.3 12.5 %copy-start.6 = (bf16[1024,4224]{1,0:T(8,128)(2,1)S(1)}, bf16[1024,4224]{1,0:T(8,128)(2,1)}, u32[]{:S(2)}) copy-start(bf16[1024,4224]{1,0:T(8,128)(2,1)} %all-gather.5.cloned.1.call-done) | copy-start | bytes 25952260
  468.3 24.7 %slice-start.2 = ((s8[7340032]{0:T(1024)(128)(4,1)}), s8[4194304]{0:T(1024)(128)(4,1)S(1)}, s32[]{:S(2)}) async-start(s8[7340032]{0:T(1024)(128)(4,1)} %bitcast.67), calls=%async_computation.8 | async-start | bytes 8388608
  480.9 12.0 %slice-start.3 = ((s8[7340032]{0:T(1024)(128)(4,1)}), s8[3145728]{0:T(1024)(128)(4,1)S(1)}, s32[]{:S(2)}) async-start(s8[7340032]{0:T(1024)(128)(4,1)} %bitcast.67), calls=%async_computation.9 | async-start | bytes 6291456
  493.0 220.9 %copy-start.1 = (f32[1,4096,4]{1,2,0:T(4,128)S(1)}, f32[1,4096,4]{1,2,0:T(4,128)}, u32[]{:S(2)}) copy-start(f32[1,4096,4]{1,2,0:T(4,128)} %param.12) | copy-start | bytes 196612
  684.6 28.5 %collective-permute-start.1 = (bf16[32,4096]{1,0:T(8,128)(2,1)S(1)}, bf16[32,4096]{1,0:T(8,128)(2,1)S(1)}, u32[]{:S(2)}, u32[]{:S(2)}) collective-permute-start(bf16[32,4096]{1,0:T(8,128)(2,1)S(1)} %fusion.36), channel_id=1, source_target_pairs={{0,32},{32,64},{64,96},{96,0},{1,33},{33,65},{65,97},{97,1},{2,34}... | collective-permute-start | bytes 786440 | tf_op jit(solution)/shard_map/ppermute | solution.py:14
Sparse Core Ops, SparseCore 0:
  11.9 107.7 all-gather.2
  156.6 178.7 reduce-scatter.2
  366.9 101.3 all-gather.4
  504.2 179.2 reduce-scatter.4

commit v2 on v1

v2 whole, which is shorter than its diff:
```python
import jax
import jax.numpy as jnp
from jax import lax
from jax.experimental import pallas as pl
from jax.experimental.pallas import tpu as pltpu
from jax.sharding import PartitionSpec as P

EXPERTS = 4
STEPS = 2
EXTRA = 128
BLOCK = 16
LANE = 128

epsilon = 1e-05

OWN, PLUS, MINUS, FAR = 0, 1, 2, 3
SLAB = (
    {OWN: 0, PLUS: 2, MINUS: 3, FAR: 6},
    {OWN: 1, PLUS: 4, MINUS: 5, FAR: 7},
)


def row_of(color, last, half, middle):
    return SLAB[color][last] * 128 + half * 64 + middle * 16


def shifted(x, axis, by):
    size = lax.axis_size(axis)
    return lax.ppermute(x, axis, [(i, (i + by) % size) for i in range(size)])


BUNDLES = ((0, OWN), (0, MINUS), (0, PLUS), (1, OWN), (0, FAR), (1, MINUS), (1, PLUS), (1, FAR))


def step_kernel(
    packed_ref, x_ref, gate_hbm, up_hbm, down_hbm, out_ref,
    rows, wide, down, hidden, part, ring_last, ring_mid, y_in, share,
    send_sems, recv_sems, load_sems,
):
    width = x_ref.shape[1]
    half_w = width // 2
    full = packed_ref.shape[1]
    ff = down.shape[0]
    tiles = ff // LANE
    section = lax.axis_index("section")
    e = lax.axis_index("expert")
    cx, cy, cz = e // 8, (e // 4) % 2, e % 4

    def at(x, y, z):
        return {"section": section, "expert": x * 8 + y * 4 + z}

    x_up = at(lax.rem(cx + 1, 4), cy, cz)
    x_dn = at(lax.rem(cx + 3, 4), cy, cz)
    z_up = at(cx, cy, lax.rem(cz + 1, 4))
    z_dn = at(cx, cy, lax.rem(cz + 3, 4))
    partner = at(cx, 1 - cy, cz)
    mid_to = ((x_up, x_dn), (z_up, z_dn))
    last_to = ((z_up, z_dn), (x_up, x_dn))

    loads = []

    def load(src, dst):
        copy = pltpu.make_async_copy(src, dst, load_sems.at[len(loads)])
        copy.start()
        loads.append(copy)

    for j in range(tiles):
        load(gate_hbm.at[:, pl.ds(j * LANE, LANE)], wide.at[j, :, pl.ds(0, LANE)])
        load(up_hbm.at[:, pl.ds(j * LANE, LANE)], wide.at[j, :, pl.ds(LANE, LANE)])
    load(down_hbm, down)

    barrier = pltpu.get_barrier_semaphore()
    for device in (x_up, x_dn, z_up, z_dn, partner):
        pl.semaphore_signal(barrier, inc=1, device_id=device, device_id_type=pl.DeviceIdType.MESH)
    pl.semaphore_wait(barrier, 5)

    sent = []
    coming = {}

    def send(key, src, dst, device):
        n = len(sent)
        copy = pltpu.make_async_remote_copy(
            src_ref=src, dst_ref=dst, send_sem=send_sems.at[n], recv_sem=recv_sems.at[n],
            device_id=device, device_id_type=pl.DeviceIdType.MESH,
        )
        copy.start()
        sent.append(copy)
        coming[key] = copy

    def arrive(key):
        coming[key].wait_recv()

    left = (pl.ds(0, half_w), pl.ds(half_w, full - half_w))

    def block(color, last, half, middle):
        return pl.ds(row_of(color, last, half, middle), BLOCK)

    def along_mid(c, half):
        for way, slot in ((0, MINUS), (1, PLUS)):
            src = (
                packed_ref.at[pl.ds(c * BLOCK, BLOCK)]
                if half == 0
                else rows.at[block(c, OWN, 1, OWN)]
            )
            send(("mid", c, half, way), src, rows.at[block(c, OWN, half, slot)], mid_to[c][way])

    def forward_mid(c, half, way):
        slot = (MINUS, PLUS)[way]
        send(
            ("midfar", c, half, way),
            rows.at[block(c, OWN, half, slot), left[way]],
            rows.at[block(c, OWN, half, FAR), left[way]],
            mid_to[c][way],
        )

    def along_last(c, k):
        half, middle = BUNDLES[k]
        src = (
            packed_ref.at[pl.ds(c * BLOCK, BLOCK)]
            if k == 0
            else rows.at[block(c, OWN, half, middle)]
        )
        for way, slot in ((0, MINUS), (1, PLUS)):
            send(("last", c, k, way), src, rows.at[block(c, slot, half, middle)], last_to[c][way])

    def forward_last(c, k, way):
        half, middle = BUNDLES[k]
        slot = (MINUS, PLUS)[way]
        send(
            ("lastfar", c, k, way),
            rows.at[block(c, slot, half, middle), left[way]],
            rows.at[block(c, FAR, half, middle), left[way]],
            last_to[c][way],
        )

    for c in (0, 1):
        along_mid(c, 0)
        send(
            ("y", c), packed_ref.at[pl.ds(c * BLOCK, BLOCK)], rows.at[block(c, OWN, 1, OWN)], partner
        )
    for c in (0, 1):
        along_last(c, 0)
    for c in (0, 1):
        rows[block(c, OWN, 0, OWN), :] = packed_ref[pl.ds(c * BLOCK, BLOCK), :]

    def pass_last(k):
        for c in (0, 1):
            for way in (0, 1):
                arrive(("last", c, k, way))
                forward_last(c, k, way)

    for way, k in ((0, 1), (1, 2)):
        for c in (0, 1):
            arrive(("mid", c, 0, way))
            forward_mid(c, 0, way)
            along_last(c, k)
    for c in (0, 1):
        arrive(("y", c))
        along_mid(c, 1)
        along_last(c, 3)
    pass_last(0)
    for c in (0, 1):
        for way in (0, 1):
            arrive(("midfar", c, 0, way))
        along_last(c, 4)
    pass_last(1)
    for way, k in ((0, 5), (1, 6)):
        for c in (0, 1):
            arrive(("mid", c, 1, way))
            forward_mid(c, 1, way)
            along_last(c, k)
    pass_last(2)
    for c in (0, 1):
        for way in (0, 1):
            arrive(("midfar", c, 1, way))
        along_last(c, 7)

    def make_hidden(s):
        @pl.loop(0, tiles)
        def _(j):
            both = jnp.dot(
                rows[pl.ds(s * 256, 256), pl.ds(0, width)], wide[j],
                preferred_element_type=jnp.float32,
            )
            gate = both[:, :LANE]
            value = gate / (1.0 + jnp.exp(-gate)) * both[:, LANE:]
            hidden[pl.ds(s * 256, 256), pl.ds(pl.multiple_of(j * LANE, LANE), LANE)] = value.astype(
                jnp.bfloat16
            )

    lanes = lax.broadcasted_iota(jnp.int32, (256, EXTRA), 1)

    def make_part(s):
        tags = rows[pl.ds(s * 256, 256), pl.ds(width, EXTRA)].astype(jnp.float32)
        share[...] = jnp.sum(jnp.where(lanes == cx, tags, 0.0), 1, keepdims=True)

        @pl.loop(0, width // 512)
        def _(j):
            cols = pl.ds(pl.multiple_of(j * 512, 512), 512)
            value = jnp.dot(
                hidden[pl.ds(s * 256, 256), :], down[:, cols], preferred_element_type=jnp.float32
            )
            part[pl.ds(s * 256, 256), cols] = (value * share[...]).astype(jnp.bfloat16)

    for copy in loads[:-1]:
        copy.wait()
    make_hidden(0)
    loads[-1].wait()
    for k in range(3, 8):
        pass_last(k)

    sides = (pl.ds(0, half_w), pl.ds(half_w, half_w))

    def reduce_send(stage, c, half, way, kind):
        near = (PLUS, MINUS)[way]
        target = FAR if kind == 1 else near
        side = sides[1 - way] if kind == 0 else sides[way]
        if stage == "last":
            src = part.at[pl.ds(row_of(c, target, half, OWN), 64), side]
            dst = ring_last.at[c, half, way, kind]
            device = last_to[c][way]
        else:
            src = part.at[block(c, OWN, half, target), side]
            dst = ring_mid.at[c, half, way, kind]
            device = mid_to[c][way]
        send((stage, c, half, way, kind, "r"), src, dst, device)

    def reduce_pass(stage, c, half, way):
        arrive((stage, c, half, way, 1, "r"))
        near = (PLUS, MINUS)[way]
        side = sides[way]
        count = 4 if stage == "last" else 1
        base = row_of(c, near, half, OWN) if stage == "last" else row_of(c, OWN, half, near)
        landed = (ring_last if stage == "last" else ring_mid).at[c, half, way, 1]

        @pl.loop(0, count)
        def _(i):
            off = pl.multiple_of(i * BLOCK, BLOCK)
            here = pl.ds(pl.multiple_of(base + off, BLOCK), BLOCK)
            total = part[here, side].astype(jnp.float32) + landed[pl.ds(off, BLOCK), :].astype(
                jnp.float32
            )
            part[here, side] = total.astype(jnp.bfloat16)

        reduce_send(stage, c, half, way, 2)

    def reduce_end(stage, c, half):
        for way in (0, 1):
            arrive((stage, c, half, way, 0, "r"))
            arrive((stage, c, half, way, 2, "r"))
        count = 4 if stage == "last" else 1
        base = row_of(c, OWN, half, OWN)
        landed = (ring_last if stage == "last" else ring_mid).at[c, half]

        @pl.loop(0, count)
        def _(i):
            off = pl.multiple_of(i * BLOCK, BLOCK)
            here = pl.ds(pl.multiple_of(base + off, BLOCK), BLOCK)
            for way in (0, 1):
                total = (
                    part[here, sides[way]].astype(jnp.float32)
                    + landed[1 - way, 0, pl.ds(off, BLOCK), :].astype(jnp.float32)
                    + landed[way, 2, pl.ds(off, BLOCK), :].astype(jnp.float32)
                )
                part[here, sides[way]] = total.astype(jnp.bfloat16)

    make_hidden(1)
    make_part(1)
    for half in (1, 0):
        for way in (0, 1):
            reduce_send("last", 0, half, way, 0)
    make_hidden(2)
    make_part(2)
    for half in (1, 0):
        for way in (0, 1):
            reduce_send("last", 1, half, way, 0)
    for k in range(8):
        for c in (0, 1):
            for way in (0, 1):
                arrive(("lastfar", c, k, way))
    make_hidden(3)
    make_part(3)
    for half in (1, 0):
        for c in (0, 1):
            for way in (0, 1):
                reduce_send("last", c, half, way, 1)
    make_part(0)
    for half in (1, 0):
        for c in (0, 1):
            for way in (0, 1):
                reduce_pass("last", c, half, way)
    for half in (1, 0):
        for c in (0, 1):
            reduce_end("last", c, half)
            for way in (0, 1):
                reduce_send("mid", c, half, way, 1)
            for way in (0, 1):
                reduce_send("mid", c, half, way, 0)
    for half in (1, 0):
        for c in (0, 1):
            for way in (0, 1):
                reduce_pass("mid", c, half, way)
    for c in (0, 1):
        reduce_end("mid", c, 1)
        send(("ysum", c), part.at[block(c, OWN, 1, OWN)], y_in.at[c], partner)
    for c in (0, 1):
        reduce_end("mid", c, 0)
    for c in (0, 1):
        arrive(("ysum", c))
        here = pl.ds(c * BLOCK, BLOCK)
        total = (
            x_ref[here, :].astype(jnp.float32)
            + part[block(c, OWN, 0, OWN), :].astype(jnp.float32)
            + y_in[c].astype(jnp.float32)
        )
        out_ref[here, :] = total.astype(jnp.bfloat16)
    for copy in sent:
        copy.wait_send()


def copies_count():
    gather = 2 * (1 + 2 * 4 + 8 * 4)
    reduce = 2 * (2 * 2 * 3 + 2 * 2 * 3 + 1)
    return gather + reduce


def expert_step(packed, activation, gate_cols, up_cols, down_rows):
    tokens, width = activation.shape
    ff = gate_cols.shape[1]
    bf16 = jnp.bfloat16
    total = 1024
    return pl.pallas_call(
        step_kernel,
        out_shape=jax.ShapeDtypeStruct((tokens, width), bf16),
        in_specs=[pl.BlockSpec(memory_space=pltpu.VMEM)] * 2
        + [pl.BlockSpec(memory_space=pl.ANY)] * 3,
        out_specs=pl.BlockSpec(memory_space=pltpu.VMEM),
        scratch_shapes=[
            pltpu.VMEM((total, width + EXTRA), bf16),
            pltpu.VMEM((ff // LANE, width, 2 * LANE), bf16),
            pltpu.VMEM((ff, width), bf16),
            pltpu.VMEM((total, ff), bf16),
            pltpu.VMEM((total, width), bf16),
            pltpu.VMEM((2, 2, 2, 3, 64, width // 2), bf16),
            pltpu.VMEM((2, 2, 2, 3, BLOCK, width // 2), bf16),
            pltpu.VMEM((2, BLOCK, width), bf16),
            pltpu.VMEM((256, 1), jnp.float32),
            pltpu.SemaphoreType.DMA((copies_count(),)),
            pltpu.SemaphoreType.DMA((copies_count(),)),
            pltpu.SemaphoreType.DMA((2 * (ff // LANE) + 1,)),
        ],
        compiler_params=pltpu.CompilerParams(
            collective_id=0, has_side_effects=True, vmem_limit_bytes=64_000_000
        ),
        name="expert_step",
    )(packed, activation, gate_cols, up_cols, down_rows)


def moe_layer(activation, chosen, gain, router, gate_cols, up_cols, down_rows):
    as_float = activation.astype(jnp.float32)
    normed = (
        as_float
        * lax.rsqrt(jnp.mean(as_float * as_float, -1, keepdims=True) + epsilon)
        * gain
    ).astype(jnp.bfloat16)
    logits = jnp.dot(normed.astype(jnp.float32), router, precision=lax.Precision.HIGHEST)
    chooses = chosen[:, :, None] == jnp.arange(EXPERTS, dtype=jnp.int32)[None, None, :]
    picked = jnp.sum(jnp.where(chooses, logits[:, None, :], 0.0), -1)
    first_share = jax.nn.sigmoid(picked[:, 0] - picked[:, 1])
    share_pair = jnp.stack([first_share, 1.0 - first_share], 1).astype(jnp.bfloat16)
    weights = jnp.sum(jnp.where(chooses, share_pair[:, :, None].astype(jnp.float32), 0.0), 1)
    extra = jnp.pad(weights.astype(jnp.bfloat16), ((0, 0), (0, EXTRA - EXPERTS)))
    packed = jnp.concatenate([normed, extra], 1)
    return expert_step(packed, activation, gate_cols, up_cols, down_rows)


def shards(
    pending_inputs,
    arriving_microgroups,
    expert_assignment,
    segment_rescale_factor,
    assignment_logit_maps,
    gating_projections,
    expanding_projections,
    contracting_projections,
):
    section_index = lax.axis_index("section")
    present_activation = pending_inputs[0]
    records = []
    for step_index in range(STEPS):
        if step_index > 0:
            present_activation = jnp.where(
                section_index == 0, arriving_microgroups[step_index - 1], present_activation
            )
        result = moe_layer(
            present_activation,
            expert_assignment[0, step_index],
            segment_rescale_factor[0],
            assignment_logit_maps[0],
            gating_projections[0],
            expanding_projections[0],
            contracting_projections[0],
        )
        present_activation = shifted(result, "section", 1)
        records.append(present_activation)
    return jnp.stack(records)[:, None]


def solution(mesh):
    return jax.shard_map(
        shards,
        mesh=mesh,
        in_specs=(
            P("section", "expert", None),
            P(None, "expert", None),
            P("section", None, "expert", None),
            P("section", None),
            P("section", None, None),
            P("section", None, "expert"),
            P("section", None, "expert"),
            P("section", "expert", None),
        ),
        out_specs=P(None, "section", "expert", None),
        check_vma=False,
    )
```

time: 721 us -> 247 us (0.34)
  waiting for transfers between devices: 574 us -> 7.27 us
  Pallas kernels: 0 us -> 220 us
  matrix products: 72.8 us -> 1.64 us
  starting transfers between devices: 50.9 us -> 11.2 us
  between operations: 13.4 us -> 0.09 us
    reduce_scatter x2 -> x0, waiting for transfers between devices: 358 us -> none  [moe_layer(): lax.psum_scatter(output.astype(jnp.bfloat16), 'expert', scatter_dimension...]
    pallas_call x0 -> x2, Pallas kernels: none -> 220 us  [expert_step(): pl.pallas_call(step_kernel, out_shape=jax.ShapeDtypeStruct((tokens, width...]
    all_gather x2 -> x0, waiting for transfers between devices: 209 us -> none  [moe_layer(): every = lax.all_gather(packed, 'expert', axis=0, tiled=True)]
    dot_general x6 -> x0, matrix products: 71.1 us -> none  [the longest x2 25 us: moe_layer(): up_value = jnp.dot(rows, up_cols, preferred_element_type=jnp.float32)]
    ppermute x2, starting transfers between devices: 50.6 us -> 11.2 us  [shifted(): return lax.ppermute(x, axis, [(i, (i + by) % size) for i in range(size)])]
  transfers between devices with their start and end apart: 6 -> 2, of which waited for: 6 -> 2; matrix products, arithmetic and copies ran while one was open for 0% -> 0% of each run, Pallas kernels for 0% -> 0%
where the time goes in v2:
time: 247 us; the launch traced here: 246 us
  Pallas kernels  220 us (89%)
  starting transfers between devices  11.2 us (5%)
  waiting for transfers between devices  7.27 us (3%)
  other arithmetic  5.05 us (2%)
    pallas_call x2, Pallas kernels, expert_step(): pl.pallas_call(step_kernel, out_shape=jax.ShapeDtypeStruct((tokens, width...  220 us
    ppermute x2, starting transfers between devices, shifted(): return lax.ppermute(x, axis, [(i, (i + by) % size) for i in range(size)])  11.2 us
    ppermute x2, waiting for transfers between devices, shifted(): return lax.ppermute(x, axis, [(i, (i + by) % size) for i in range(size)])  7.27 us
  transfers between devices with their start and end apart: 2, of which 2 were waited for; matrix products, arithmetic and copies ran while one was open for 0% of the time, Pallas kernels for 0%

profile of v2, /device:TPU:1, one launch (start us, length us, event | category | flops | bytes accessed | tf_op | source)
XLA Modules:
  0.0 245.8 jit_solution(814351409718394892)
XLA Ops:
  0.0 0.0 copy-start
  0.0 1.1 fusion.2
  1.2 1.1 fusion.4
  2.3 0.0 copy-done
  2.3 1.3 fusion.11
  3.6 0.7 slice_bitcast_fusion
  4.4 0.1 copy.24
  4.5 0.7 fusion.8.packed_ref
  5.2 0.0 copy-start.2
  5.2 0.0 copy-start.3
  5.2 112.3 %expert_step.2 = bf16[32,4096]{1,0:T(8,128)(2,1)} custom-call(bf16[32,4224]{1,0:T(8,128)(2,1)} %fusion.8.packed_ref, bf16[32,4096]{1,0:T(8,128)(2,1)} %bitcast.35, bf16[4096,896]{1,0:T(8,128)(2,1)} %bitcast.29, bf16[4096,896]{1,0:T(8,128)(2,1)} %bitcast.31, bf16[896,4096]{1,0:T(8,128)(2,1)} %bitcast.33), custom_call_target="tpu_custom_call" | custom-call | tf_op jit(solution)/shard_map/expert_step/pallas_call | solution.py:332
  117.6 5.5 %collective-permute-start = (bf16[32,4096]{1,0:T(8,128)(2,1)}, bf16[32,4096]{1,0:T(8,128)(2,1)S(1)}, u32[]{:S(2)}, u32[]{:S(2)}) collective-permute-start(bf16[32,4096]{1,0:T(8,128)(2,1)} %expert_step.2), channel_id=1, source_target_pairs={{0,32},{32,64},{64,96},{96,0},{1,33},{33,65},{65,97},{97,1},{2,34}... | collective-permute-start | bytes 786440 | tf_op jit(solution)/shard_map/ppermute | solution.py:29
  123.1 3.6 %collective-permute-done = bf16[32,4096]{1,0:T(8,128)(2,1)S(1)} collective-permute-done((bf16[32,4096]{1,0:T(8,128)(2,1)}, bf16[32,4096]{1,0:T(8,128)(2,1)S(1)}, u32[]{:S(2)}, u32[]{:S(2)}) %collective-permute-start) | collective-permute-done | bytes 262176 | tf_op jit(solution)/shard_map/ppermute | solution.py:29
  126.7 0.0 copy-done.2
  126.7 0.2 fusion.5
  126.9 0.0 copy-start.1
  126.9 0.0 copy-done.3
  127.0 0.1 fusion.7
  127.1 0.3 fusion.15
  127.5 0.1 copy.25
  127.6 0.7 fusion.9.packed_ref
  128.3 0.0 copy-done.1
  128.3 107.3 %expert_step.3 = bf16[32,4096]{1,0:T(8,128)(2,1)} custom-call(bf16[32,4224]{1,0:T(8,128)(2,1)} %fusion.9.packed_ref, bf16[32,4096]{1,0:T(8,128)(2,1)} %copy-done.1, bf16[4096,896]{1,0:T(8,128)(2,1)} %bitcast.30, bf16[4096,896]{1,0:T(8,128)(2,1)} %bitcast.32, bf16[896,4096]{1,0:T(8,128)(2,1)} %bitcast.34), custom_call_target="tpu_custom_call" | custom-call | tf_op jit(solution)/shard_map/expert_step/pallas_call | solution.py:332
  235.6 5.7 %collective-permute-start.1 = (bf16[32,4096]{1,0:T(8,128)(2,1)}, bf16[32,4096]{1,0:T(8,128)(2,1)S(1)}, u32[]{:S(2)}, u32[]{:S(2)}) collective-permute-start(bf16[32,4096]{1,0:T(8,128)(2,1)} %expert_step.3), channel_id=1, source_target_pairs={{0,32},{32,64},{64,96},{96,0},{1,33},{33,65},{65,97},{97,1},{2,34}... | collective-permute-start | bytes 786440 | tf_op jit(solution)/shard_map/ppermute | solution.py:29
  241.3 3.6 %collective-permute-done.1 = bf16[32,4096]{1,0:T(8,128)(2,1)S(1)} collective-permute-done((bf16[32,4096]{1,0:T(8,128)(2,1)}, bf16[32,4096]{1,0:T(8,128)(2,1)S(1)}, u32[]{:S(2)}, u32[]{:S(2)}) %collective-permute-start.1) | collective-permute-done | bytes 262176 | tf_op jit(solution)/shard_map/ppermute | solution.py:29
  245.0 0.8 maximum_bitcast_fusion
  (12 shorter events, 0.2 us)
Async XLA Ops:
  0.0 2.3 copy-start
  5.2 121.5 %copy-start.2 = (bf16[1,32,4096]{2,1,0:T(8,128)(2,1)S(1)}, bf16[1,32,4096]{2,1,0:T(8,128)(2,1)}, u32[]{:S(2)}) copy-start(bf16[1,32,4096]{2,1,0:T(8,128)(2,1)} %param.9) | copy-start | bytes 786436
  5.2 121.7 %copy-start.3 = (f32[1,4096]{1,0:T(1,128)S(1)}, f32[1,4096]{1,0:T(1,128)}, u32[]{:S(2)}) copy-start(f32[1,4096]{1,0:T(1,128)} %param.11) | copy-start | bytes 49156
  117.6 9.1 %collective-permute-start = (bf16[32,4096]{1,0:T(8,128)(2,1)}, bf16[32,4096]{1,0:T(8,128)(2,1)S(1)}, u32[]{:S(2)}, u32[]{:S(2)}) collective-permute-start(bf16[32,4096]{1,0:T(8,128)(2,1)} %expert_step.2), channel_id=1, source_target_pairs={{0,32},{32,64},{64,96},{96,0},{1,33},{33,65},{65,97},{97,1},{2,34}... | collective-permute-start | bytes 786440 | tf_op jit(solution)/shard_map/ppermute | solution.py:29
  126.9 1.4 copy-start.1
  235.6 9.4 %collective-permute-start.1 = (bf16[32,4096]{1,0:T(8,128)(2,1)}, bf16[32,4096]{1,0:T(8,128)(2,1)S(1)}, u32[]{:S(2)}, u32[]{:S(2)}) collective-permute-start(bf16[32,4096]{1,0:T(8,128)(2,1)} %expert_step.3), channel_id=1, source_target_pairs={{0,32},{32,64},{64,96},{96,0},{1,33},{33,65},{65,97},{97,1},{2,34}... | collective-permute-start | bytes 786440 | tf_op jit(solution)/shard_map/ppermute | solution.py:29

commit v3 on v1

v3 whole, which is shorter than its diff:
```python
import jax
import jax.numpy as jnp
from jax import lax
from jax.experimental import pallas as pl
from jax.experimental.pallas import tpu as pltpu
from jax.sharding import PartitionSpec as P

EXPERTS = 4
STEPS = 2
EXTRA = 128
BLOCK = 16
LANE = 128
MESH = pl.DeviceIdType.MESH

epsilon = 1e-05

OWN, PLUS, MINUS, FAR = 0, 1, 2, 3
CAME = (MINUS, PLUS)
GOES = (PLUS, MINUS)
ALL = slice(None)

COLS = {"A": (0, 1024), "B": (1024, 1792), "C": (2816, 1280)}
TILE = 512

SCHEDULE = (
    (0, 1, 3, 5, 23, 25, 27, 45, 47, 151, 152, 154, 156, 174, 176, 178, 196, 198, 4, 6, 26, 28, 46, 48, 2,
     13, 15, 155, 157, 24, 35, 37, 177, 179, 197, 199, 153, 164, 166, 7, 8, 10, 29, 30, 32, 49, 50, 52, 55,
     14, 175, 16, 158, 200, 36, 38, 180, 206, 165, 167, 181, 183, 9, 11, 31, 33, 17, 18, 20, 168, 51, 53,
     56, 57, 39, 40, 42, 12, 169, 171, 19, 21, 34, 54, 58, 186, 182, 184, 188, 201, 203, 41, 43, 22, 170,
     172, 185, 187, 189, 159, 161, 44, 59,),
    (),
    (173, 190, 191, 193, 202, 204, 207,),
    (),
    (160, 162,),
    (208,),
    (205,),
    (163,),
    (192, 194, 209,),
    (60, 61, 64, 65, 77, 78, 81, 82,),
    (),
    (),
    (195, 62, 66,),
    (110, 114, 93, 94, 97, 98,),
    (),
    (79, 83, 128, 210, 132, 111, 115,),
    (126,),
    (112, 116, 63, 67,),
    (68, 69, 72, 73, 80, 84, 95, 99, 130,),
    (),
    (129, 135, 86, 90, 85, 89,),
    (),
    (133, 134, 138,),
    (),
    (70, 74, 113, 117, 118, 119, 122, 123, 211, 212, 215, 216,),
    (127, 136, 232,),
    (87, 91, 96, 71, 75, 76, 100, 101, 102, 105, 106, 120, 124,),
    (131, 139, 140, 228,),
    (261, 265, 88, 92, 229, 244, 248,),
    (),
    (107, 103, 234, 279, 245, 249, 213, 283, 125, 121, 233, 262, 266, 230, 137, 147, 142, 217, 277, 141,
     143, 146, 104, 108, 109, 263, 267, 214, 235, 280, 286, 219, 224, 231, 246, 250, 281, 218, 144, 148,
     284, 285, 289, 220, 223, 237, 241, 236, 240, 264, 268, 269, 270, 273, 221, 274, 278, 287, 247, 251,
     252, 253, 256, 257, 271, 145, 149, 150, 275, 225, 238, 242, 222, 258, 282, 254, 226, 227, 290, 291,
     239, 243, 276, 272, 302, 303, 305, 307, 325, 327, 329, 347, 349, 255, 259, 260, 288, 298, 293, 306,
     308, 292, 294, 297, 328, 348, 350, 304, 315, 317, 330, 295, 326, 337, 309, 339, 310, 312, 299, 351,
     352, 354, 357, 331, 332, 334, 316, 318, 296, 300, 301, 338, 340, 311, 313, 453, 454, 333, 335, 456,
     458, 476, 319, 320, 322, 498, 500, 478, 480, 353, 358, 355, 359, 341, 342, 344, 314, 455, 336, 477,
     488, 490, 321, 457, 323, 459, 466, 468, 499, 501, 479, 481, 356, 360, 489, 491, 343, 345, 460, 461,
     463, 324, 467, 469, 482, 483, 485, 502, 503, 505, 508, 492, 346, 493, 495, 470, 471, 473, 361,),
    (462, 464,),
    (),
    (504, 506, 509, 484, 486,),
    (510,),
    (472, 474,),
    (465,),
    (494, 496,),
    (507, 511,),
    (475, 487, 362, 366,),
    (363, 367,),
    (497,),
    (379, 383,),
    (412, 416, 380, 384,),
    (),
    (430, 395, 381, 385, 512, 399,),
    (364, 368,),
    (434, 414, 418,),
    (382, 386,),
    (365, 369, 370, 371, 374, 375,),
    (396, 400, 428, 431, 437,),
    (),
    (372, 376, 397, 401, 432, 435, 436, 440,),
    (),
    (373, 377, 413, 417, 513, 514, 517, 518, 530, 534,),
    (378, 429, 531, 535,),
    (398, 402, 388, 392, 387, 391,),
    (515, 519,),
    (563, 567, 415, 419, 433, 546, 550,),
    (532, 536, 547, 551,),
    (581, 403, 407, 585, 404, 408, 564, 568, 516, 520, 420, 424, 421, 425, 438, 441, 533, 537, 565, 569,
     579, 405, 409, 422, 426, 442, 521, 525, 522, 526, 548, 552, 583, 439, 582, 588, 406, 410, 423, 427,
     539, 543, 538, 542, 443, 586, 587, 591, 566, 570, 571, 572, 575, 523, 527, 576, 445, 449, 389, 393,
     411, 580, 444, 448, 589, 549, 553, 554, 555, 558, 559, 573, 577, 540, 544, 524, 528, 529, 390, 394,
     446, 450, 584, 592, 593, 560, 541, 545, 556, 578, 447, 451, 452, 574, 590, 600, 595, 557, 594, 596,
     599, 561, 562, 597, 601, 598, 602, 603,),
)


def kernel(
    pending_ref, arriving_ref, chosen_ref, gain_ref, router_ref, gate_hbm, up_hbm, down_hbm, out_ref,
    rows, part, wide, down, hidden, share, mine, relay,
    land_last, land_mid, land_y,
    send_sems, recv_sems, load_sems,
):
    width = pending_ref.shape[1]
    tiles = down.shape[0] // LANE
    section = lax.axis_index("section")
    e = lax.axis_index("expert")
    cx, cy, cz = e // 8, (e // 4) % 2, e % 4

    def at(x, y, z):
        return {"section": section, "expert": x * 8 + y * 4 + z}

    to_x = (at(lax.rem(cx + 1, 4), cy, cz), at(lax.rem(cx + 3, 4), cy, cz))
    to_z = (at(cx, cy, lax.rem(cz + 1, 4)), at(cx, cy, lax.rem(cz + 3, 4)))
    partner = at(cx, 1 - cy, cz)
    following = {"section": lax.rem(section + 1, 4), "expert": e}
    preceding = {"section": lax.rem(section + 3, 4), "expert": e}

    loads = []

    def load(src, dst):
        copy = pltpu.make_async_copy(src, dst, load_sems.at[len(loads)])
        copy.start()
        loads.append(copy)

    for j in range(tiles):
        load(gate_hbm.at[:, pl.ds(j * LANE, LANE)], wide.at[j, :, pl.ds(0, LANE)])
        load(up_hbm.at[:, pl.ds(j * LANE, LANE)], wide.at[j, :, pl.ds(LANE, LANE)])
    load(down_hbm, down)

    barrier = pltpu.get_barrier_semaphore()
    for device in (*to_x, *to_z, partner, following, preceding):
        pl.semaphore_signal(barrier, inc=1, device_id=device, device_id_type=MESH)

    numbers = {}
    known = {}
    flying = {}

    def send(key, group, src, dst, device):
        n = numbers.setdefault(key if "relay" in key else key[1:], len(numbers))
        known[key] = lambda: pltpu.make_async_remote_copy(
            src_ref=src(), dst_ref=dst(), send_sem=send_sems.at[n], recv_sem=recv_sems.at[n],
            device_id=device, device_id_type=MESH,
        )
        known[key]().start()
        flying.setdefault(group, []).append(known[key])

    def arrive(key):
        known[key]().wait_recv()

    def drain(group):
        for copy in flying.pop(group, []):
            copy().wait_send()

    def gathered(h, z, y, x, cols):
        return lambda: rows.at[h, z, y, x, :, cols]

    def summed(h, z, y, x, cols):
        return lambda: part.at[h, z, y, x, :, cols]

    def span(color, tags=False):
        start, size = COLS[color]
        if tags and color == "C":
            size += EXTRA
        cut = size // 2 // LANE * LANE
        return pl.ds(start, size), (pl.ds(start, cut), pl.ds(start + cut, size - cut))

    def source(s, h):
        here = pl.ds(h * BLOCK, BLOCK)
        if s == 0:
            return pending_ref[here, :].astype(jnp.float32)
        return jnp.where(section == 0, arriving_ref[here, :], relay[0, here, :]).astype(jnp.float32)

    def enter(s, h):
        here = pl.ds(h * BLOCK, BLOCK)
        value = source(s, h)
        mean = jnp.mean(value * value, -1, keepdims=True)
        normed = (value * lax.rsqrt(mean + epsilon) * gain_ref[...]).astype(jnp.bfloat16)
        rows[h, 0, 0, 0, :, pl.ds(0, width)] = normed
        precise = normed.astype(jnp.float32)
        lane = lax.broadcasted_iota(jnp.int32, (BLOCK, EXTRA), 1)
        first_choice = chosen_ref[s, here, 0:1]
        second_choice = chosen_ref[s, here, 1:2]
        gap = jnp.zeros((BLOCK, 1), jnp.float32)
        for expert in range(EXPERTS):
            logit = jnp.sum(precise * router_ref[expert : expert + 1, :], -1, keepdims=True)
            gap = gap + jnp.where(first_choice == expert, logit, 0.0)
            gap = gap - jnp.where(second_choice == expert, logit, 0.0)
        first = 1.0 / (1.0 + jnp.exp(-gap))
        second = 1.0 - first
        tags = jnp.where(lane == first_choice, first, 0.0) + jnp.where(
            lane == second_choice, second, 0.0
        )
        rows[h, 0, 0, 0, :, pl.ds(width, EXTRA)] = tags.astype(jnp.bfloat16)

    events = {}

    def event(s, h, label, keys, needs, act):
        def run():
            for key in keys:
                arrive(key)
            act()

        events[s, h, label] = Event(keys, needs, run)

    def gather(s, h):
        group = ("g", s, h)

        def key(tag, way=0):
            return (s, h, "g", tag, way)

        def near(tag, color, to, place, way):
            cols = span(color, True)[0]
            send(key(tag, way), group, gathered(h, *place(OWN), cols),
                 gathered(h, *place(CAME[way]), cols), to[way])

        def ring(tag, color, to, place, needs):
            sides = span(color, True)[1]
            for way in (0, 1):
                event(s, h, (tag, "n", way), [], needs,
                      lambda way=way: near(tag, color, to, place, way))

                def forward(way=way):
                    send(key(tag + "f", way), group, gathered(h, *place(CAME[way]), sides[way]),
                         gathered(h, *place(FAR), sides[way]), to[way])

                event(s, h, (tag, "f", way), [key(tag, way)], [(tag, "n", way)], forward)
            event(s, h, (tag, "e", 0), [key(tag + "f", 0), key(tag + "f", 1)],
                  [(tag, "f", 0), (tag, "f", 1)], lambda: None)
            return (tag, "e", 0)

        def across(tag, color, z, x, needs):
            cols = span(color, True)[0]
            event(s, h, (tag, "n", 0), [], needs, lambda: send(
                key(tag), group, gathered(h, z, 0, x, cols), gathered(h, z, 1, x, cols), partner))
            return key(tag)

        ready = ("enter", "e", 0)
        before = [(s - 1, h, "r", "relay", 0)] if s else []
        event(s, h, ready, before, [("sum", "e", 0)] if s else [], lambda: enter(s, h))
        finals, ends = [], []
        for color in "AB":
            to_mid, to_last = (to_x, to_z) if color == "A" else (to_z, to_x)
            crossed = across(color + "y", color, OWN, OWN, [ready])
            event(s, h, (color + "y", "e", 0), [crossed], [(color + "y", "n", 0)], lambda: None)
            for y in (0, 1):
                mid = (lambda p, y=y: (OWN, y, p)) if color == "A" else (lambda p, y=y: (p, y, OWN))
                last = (lambda p, y=y: (p, y, ALL)) if color == "A" else (lambda p, y=y: (ALL, y, p))
                end = ring(f"{color}m{y}", color, to_mid, mid, [(color + "y", "e", 0) if y else ready])
                ends.append(ring(f"{color}l{y}", color, to_last, last, [end]))
        end_x = ring("Cx", "C", to_x, lambda p: (OWN, 0, p), [ready])
        end_z = ring("Cz", "C", to_z, lambda p: (p, 0, ALL), [end_x])
        for place, need in ((OWN, end_x), (MINUS, ("Cz", "f", 0)), (PLUS, ("Cz", "f", 1)), (FAR, end_z)):
            finals.append(across(f"Cy{place}", "C", place, ALL, [need]))
        event(s, h, ("gathered", "e", 0), finals, ends + [end_z] + [(f"Cy{p}", "n", 0) for p in range(4)],
              lambda: None)

    def reduce(s, h):
        group = ("r", s, h)

        def key(tag, way=0, kind=0):
            return (s, h, "r", tag, way, kind)

        def ring(tag, color, to, place, landing, needs):
            sides = span(color)[1]

            def go(way, kind):
                target = FAR if kind == 1 else GOES[way]
                side = sides[1 - way] if kind == 0 else sides[way]
                send(key(tag, way, kind), group, summed(h, *place(target), side),
                     lambda: landing(way, kind), to[way])

            for way in (0, 1):
                event(s, h, (tag, "s", way), [], needs[way], lambda way=way: go(way, 1))
                event(s, h, (tag, "d", way), [], needs[1 - way], lambda way=way: go(way, 0))

                def onward(way=way):
                    here = summed(h, *place(GOES[way]), sides[way])()
                    total = here[...].astype(jnp.float32) + landing(way, 1)[...].astype(jnp.float32)
                    here[...] = total.astype(jnp.bfloat16)
                    go(way, 2)

                event(s, h, (tag, "p", way), [key(tag, way, 1)], [(tag, "s", way)] + needs[way], onward)

                def finish(way=way):
                    here = summed(h, *place(OWN), sides[way])()
                    total = (
                        here[...].astype(jnp.float32)
                        + landing(1 - way, 0)[...].astype(jnp.float32)
                        + landing(way, 2)[...].astype(jnp.float32)
                    )
                    here[...] = total.astype(jnp.bfloat16)

                event(s, h, (tag, "t", way), [key(tag, 1 - way, 0), key(tag, way, 2)],
                      [(tag, "d", 1 - way), (tag, "p", way)], finish)
            return [[(tag, "t", 0)], [(tag, "t", 1)]]

        def half_cols(color):
            start, size = COLS[color]
            return pl.ds(start // 2, size // 2)

        finals, arrivals = [], []
        for color in "AB":
            to_mid, to_last = (to_x, to_z) if color == "A" else (to_z, to_x)
            cols = span(color)[0]
            tile = [("tile", color, 0)]
            for y in (1, 0):
                mid = (lambda p, y=y: (OWN, y, p)) if color == "A" else (lambda p, y=y: (p, y, OWN))
                last = (lambda p, y=y: (p, y, ALL)) if color == "A" else (lambda p, y=y: (ALL, y, p))
                ends = ring(
                    f"{color}L{y}", color, to_last, last,
                    lambda way, kind, y=y, color=color: land_last.at[h, y, way, kind, :, :, half_cols(color)],
                    [tile, tile],
                )
                ends = ring(
                    f"{color}M{y}", color, to_mid, mid,
                    lambda way, kind, y=y, color=color: land_mid.at[h, y, way, kind, :, half_cols(color)],
                    ends,
                )
                if y == 1:
                    event(s, h, (color + "Y", "n", 0), [], ends[0] + ends[1], lambda color=color, cols=cols: send(
                        key(color + "Y"), group, summed(h, OWN, 1, OWN, cols),
                        lambda: land_y.at[h, 0, 0, :, cols], partner))
                    finals.append((color + "Y", "n", 0))
                    arrivals.append(key(color + "Y"))
                else:
                    finals += ends[0] + ends[1]
        c_cols = span("C")[0]
        for z in range(4):
            event(s, h, (f"CY{z}", "n", 0), [], [("tile", "C", 0)], lambda z=z: send(
                key("CY", z), group, summed(h, z, 1, ALL, c_cols),
                lambda: land_y.at[h, z, :, :, c_cols], partner))

            def add(z=z):
                here = part.at[h, z, 0, :, :, c_cols]
                total = here[...].astype(jnp.float32) + land_y[h, z, :, :, c_cols].astype(jnp.float32)
                here[...] = total.astype(jnp.bfloat16)

            event(s, h, (f"CY{z}", "a", 0), [key("CY", z)], [(f"CY{z}", "n", 0)], add)
        all_z = [(f"CY{z}", "a", 0) for z in range(4)]
        ends = ring("CZ", "C", to_z, lambda p: (p, 0, ALL),
                    lambda way, kind: land_last.at[h, 0, way, kind, :, :, half_cols("C")], [all_z, all_z])
        for way in (0, 1):
            near = (f"CY{GOES[way]}", "a", 0)
            events[s, h, ("CZ", "s", way)].needs[:] = [(f"CY{FAR}", "a", 0)]
            events[s, h, ("CZ", "d", way)].needs[:] = [near]
            events[s, h, ("CZ", "p", way)].needs[:] = [("CZ", "s", way), near]
            events[s, h, ("CZ", "t", way)].needs.append((f"CY{OWN}", "a", 0))
        ends = ring("CX", "C", to_x, lambda p: (OWN, 0, p),
                    lambda way, kind: land_mid.at[h, 0, way, kind, :, half_cols("C")], ends)
        finals += ends[0] + ends[1]

        def total_of():
            here = pl.ds(h * BLOCK, BLOCK)
            total = source(s, h) + part[h, 0, 0, 0, :, :].astype(jnp.float32)
            ab = pl.ds(0, COLS["C"][0])
            mine[s, here, ab] = (
                total[:, : COLS["C"][0]] + land_y[h, 0, 0, :, ab].astype(jnp.float32)
            ).astype(jnp.bfloat16)
            mine[s, here, c_cols] = total[:, COLS["C"][0] :].astype(jnp.bfloat16)
            send((s, h, "r", "relay", 0), "relay", lambda: mine.at[s, here, :],
                 lambda: relay.at[s, here, :], following)

        event(s, h, ("sum", "e", 0), arrivals, finals, total_of)

    lanes = lax.broadcasted_iota(jnp.int32, (512, EXTRA), 1)

    def hidden_tile(h, j):
        both = jnp.dot(
            rows[h, :, :, :, :, pl.ds(0, width)].reshape(512, width), wide[j],
            preferred_element_type=jnp.float32,
        )
        gate = both[:, :LANE]
        value = gate / (1.0 + jnp.exp(-gate)) * both[:, LANE:]
        hidden[:, pl.ds(pl.multiple_of(j * LANE, LANE), LANE)] = value.astype(jnp.bfloat16)

    def start_part(s, h):
        tags = rows[h, :, :, :, :, pl.ds(width, EXTRA)].reshape(512, EXTRA).astype(jnp.float32)
        share[...] = jnp.sum(jnp.where(lanes == cx, tags, 0.0), 1, keepdims=True)
        drain(("g", s, h))
        drain(("r", s - 1, h))

    def part_tile(h, j):
        cols = pl.ds(pl.multiple_of(j * TILE, TILE), TILE)
        value = jnp.dot(hidden[...], down[:, cols], preferred_element_type=jnp.float32)
        value = (value * share[...]).astype(jnp.bfloat16)
        part[h, :, :, :, :, cols] = value.reshape(4, 2, 4, BLOCK, TILE)

    def finish_all():
        for s in range(STEPS):
            if s == STEPS - 1:
                for h in (0, 1):
                    arrive((s, h, "r", "relay", 0))
            out_ref[s] = relay[s]
        for group in list(flying):
            drain(group)

    for s in range(STEPS):
        for h in (0, 1):
            gather(s, h)
            reduce(s, h)

    replay(
        events, pl.semaphore_wait, barrier, loads, hidden_tile, start_part, part_tile, finish_all,
        tiles, width // TILE,
    )


class Event:
    def __init__(self, keys, needs, run):
        self.keys, self.needs, self.run = keys, list(needs), run


def replay(events, wait, barrier, loads, hidden_tile, start_part, part_tile, finish_all, tiles, ticks):
    names = list(events)
    slots = iter(SCHEDULE)

    def now():
        for n in next(slots):
            events[names[n]].run()

    wait(barrier, 7)
    now()
    for copy in loads:
        copy.wait()
    for s in range(STEPS):
        for h in (0, 1):
            table = [next(slots) for _ in range(tiles + ticks)]

            def during(j, entries):
                for tick, numbers in enumerate(entries):
                    if numbers:
                        @pl.when(j == tick)
                        def _(numbers=numbers):
                            for n in numbers:
                                events[names[n]].run()

            @pl.loop(0, tiles)
            def _(j):
                hidden_tile(h, j)
                during(j, table[:tiles])

            start_part(s, h)

            @pl.loop(0, ticks)
            def _(j):
                part_tile(h, j)
                during(j, table[tiles:])

    finish_all()


def both_steps(pending, arriving, chosen, gain, router, gate_cols, up_cols, down_rows):
    tokens, width = pending.shape
    ff = gate_cols.shape[1]
    bf16 = jnp.bfloat16
    copies = 2 * (2 * 17 + 12 + 2 * 25 + 16 + 2)
    return pl.pallas_call(
        kernel,
        out_shape=jax.ShapeDtypeStruct((STEPS, tokens, width), bf16),
        in_specs=[pl.BlockSpec(memory_space=pltpu.VMEM)] * 5
        + [pl.BlockSpec(memory_space=pl.ANY)] * 3,
        out_specs=pl.BlockSpec(memory_space=pltpu.VMEM),
        scratch_shapes=[
            pltpu.VMEM((2, 4, 2, 4, BLOCK, width + EXTRA), bf16),
            pltpu.VMEM((2, 4, 2, 4, BLOCK, width), bf16),
            pltpu.VMEM((ff // LANE, width, 2 * LANE), bf16),
            pltpu.VMEM((ff, width), bf16),
            pltpu.VMEM((512, ff), bf16),
            pltpu.VMEM((512, 1), jnp.float32),
            pltpu.VMEM((STEPS, tokens, width), bf16),
            pltpu.VMEM((STEPS, tokens, width), bf16),
            pltpu.VMEM((2, 2, 2, 3, 4, BLOCK, width // 2), bf16),
            pltpu.VMEM((2, 2, 2, 3, BLOCK, width // 2), bf16),
            pltpu.VMEM((2, 4, 4, BLOCK, width), bf16),
            pltpu.SemaphoreType.DMA((copies,)),
            pltpu.SemaphoreType.DMA((copies,)),
            pltpu.SemaphoreType.DMA((2 * (ff // LANE) + 1,)),
        ],
        compiler_params=pltpu.CompilerParams(
            collective_id=0, has_side_effects=True, vmem_limit_bytes=66_000_000
        ),
        name="both_steps",
    )(pending, arriving, chosen, gain, router, gate_cols, up_cols, down_rows)


def shards(
    pending_inputs,
    arriving_microgroups,
    expert_assignment,
    segment_rescale_factor,
    assignment_logit_maps,
    gating_projections,
    expanding_projections,
    contracting_projections,
):
    carried = both_steps(
        pending_inputs[0],
        arriving_microgroups[0],
        expert_assignment[0],
        segment_rescale_factor,
        assignment_logit_maps[0].T,
        gating_projections[0],
        expanding_projections[0],
        contracting_projections[0],
    )
    return carried[:, None]


def solution(mesh):
    return jax.shard_map(
        shards,
        mesh=mesh,
        in_specs=(
            P("section", "expert", None),
            P(None, "expert", None),
            P("section", None, "expert", None),
            P("section", None),
            P("section", None, None),
            P("section", None, "expert"),
            P("section", None, "expert"),
            P("section", "expert", None),
        ),
        out_specs=P(None, "section", "expert", None),
        check_vma=False,
    )
```

time: 721 us -> 208 us (0.29)
  waiting for transfers between devices: 574 us -> 0 us
  Pallas kernels: 0 us -> 204 us
  matrix products: 72.8 us -> 0 us
  starting transfers between devices: 50.9 us -> 0 us
  between operations: 13.4 us -> 0.01 us
  other arithmetic: 8.33 us -> 0 us
    reduce_scatter x2 -> x0, waiting for transfers between devices: 358 us -> none  [moe_layer(): lax.psum_scatter(output.astype(jnp.bfloat16), 'expert', scatter_dimension...]
    all_gather x2 -> x0, waiting for transfers between devices: 209 us -> none  [moe_layer(): every = lax.all_gather(packed, 'expert', axis=0, tiled=True)]
    pallas_call x0 -> x1, Pallas kernels: none -> 204 us  [both_steps(): pl.pallas_call(kernel, out_shape=jax.ShapeDtypeStruct((STEPS, tokens, wid...]
    dot_general x8 -> x0, matrix products: 72.8 us -> none  [the longest x2 25 us: moe_layer(): up_value = jnp.dot(rows, up_cols, preferred_element_type=jnp.float32)]
    ppermute x2 -> x0, starting transfers between devices: 50.6 us -> none  [shifted(): return lax.ppermute(x, axis, [(i, (i + by) % size) for i in range(size)])]
  transfers between devices with their start and end apart: 6 -> 0, of which waited for: 6 -> 0; matrix products, arithmetic and copies ran while one was open for 0% -> 0% of each run, Pallas kernels for 0% -> 0%
where the time goes in v3:
time: 208 us
  Pallas kernels  204 us (98%)
  local copies, waits for them, and re-layouts  3.25 us (2%)
    pallas_call x1, Pallas kernels, both_steps(): pl.pallas_call(kernel, out_shape=jax.ShapeDtypeStruct((STEPS, tokens, wid...  204 us

profile of v3, /device:TPU:1, one launch (start us, length us, event | category | flops | bytes accessed | tf_op | source)
XLA Modules:
  0.0 207.7 jit_solution(9227484976065219864)
XLA Ops:
  0.0 1.4 copy.9.chosen_ref
  1.4 204.4 %both_steps.1 = bf16[2,32,4096]{2,1,0:T(8,128)(2,1)} custom-call(bf16[32,4096]{1,0:T(8,128)(2,1)} %bitcast.16, bf16[32,4096]{1,0:T(8,128)(2,1)} %bitcast.17, s32[2,32,2]{2,1,0:T(8,128)} %copy.9.chosen_ref, f32[1,4096]{1,0:T(1,128)} %gain_ref.1, f32[4,4096]{1,0:T(4,128)} %bitcast.18, bf16[4096,896]{1,0:T(8,128)(2,1)} %bitcast.12, bf16[4096,896]{1,0:T(8,128)(2,1)} %bitcast.13, ...), custom_call_target="tpu_custom_call" | custom-call | tf_op jit(solution)/shard_map/both_steps/pallas_call | solution.py:468
  205.8 1.9 copy.12

commit v4 on v3

--- a/solution.py
+++ b/solution.py
@@ -19,89 +19,103 @@
 GOES = (PLUS, MINUS)
 ALL = slice(None)
 
-COLS = {"A": (0, 1024), "B": (1024, 1792), "C": (2816, 1280)}
+COLS = {"A": (1024, 1024), "B": (2048, 2048), "C": (0, 1024)}
+TAGGED = "C"
 TILE = 512
 
+GATHER_PIECES = (("o", OWN), ("n", slice(PLUS, FAR)), ("f", FAR))
+REDUCE_PIECES = (("n", slice(OWN, FAR)), ("f", FAR))
+
 SCHEDULE = (
-    (0, 1, 3, 5, 23, 25, 27, 45, 47, 151, 152, 154, 156, 174, 176, 178, 196, 198, 4, 6, 26, 28, 46, 48, 2,
-     13, 15, 155, 157, 24, 35, 37, 177, 179, 197, 199, 153, 164, 166, 7, 8, 10, 29, 30, 32, 49, 50, 52, 55,
-     14, 175, 16, 158, 200, 36, 38, 180, 206, 165, 167, 181, 183, 9, 11, 31, 33, 17, 18, 20, 168, 51, 53,
-     56, 57, 39, 40, 42, 12, 169, 171, 19, 21, 34, 54, 58, 186, 182, 184, 188, 201, 203, 41, 43, 22, 170,
-     172, 185, 187, 189, 159, 161, 44, 59,),
+    (0, 85, 87, 90, 92, 1, 8, 10, 43, 45, 47, 50, 52, 241, 326, 328, 242, 3, 5, 284, 331, 333, 291, 293,
+     249, 251, 86, 88, 91, 93, 95, 97, 9, 11, 244, 246, 2, 23, 25, 28, 30, 51, 53, 46, 48, 55, 57, 44, 65,
+     67, 70, 72, 4, 6, 13, 15, 243, 94, 89, 100, 102, 105, 285, 96, 98, 12, 24, 26, 33, 35, 29, 31, 54, 49,
+     60, 62, 66, 68, 75, 77, 56, 58, 14, 16, 101, 106, 71, 103, 107, 73, 7, 18, 20, 27, 38, 40, 99, 34, 61,
+     63, 36, 32, 332, 250, 334, 69, 80, 82, 286, 252, 288, 17, 104, 108, 19, 76, 78, 306, 21, 39, 308, 41,
+     59, 37, 269, 327, 335, 74, 329, 245, 253, 338, 247, 336, 264, 64, 266, 311, 313, 256, 81, 22, 83, 254,
+     289, 292, 79, 287, 298, 42, 330, 346, 343, 296, 341, 248, 261, 259, 339, 337, 309, 267, 270, 314, 307,
+     265, 257, 84, 109,),
+    (344, 342, 347, 255, 274, 276, 290, 301, 303,),
+    (340, 260, 262, 299, 312, 316, 271,),
+    (348, 268, 279, 281, 310, 318,),
+    (345, 258, 297,),
+    (349, 263, 272, 275, 277, 302, 304, 315, 323,),
+    (280, 282, 321, 294,),
+    (273, 317, 319,),
+    (278, 300, 305,),
+    (283, 324, 208,),
+    (295, 322, 210,),
+    (110, 114, 320, 118, 122, 111, 115, 119, 123,),
+    (136, 140, 143, 147,),
+    (212, 325, 350, 144, 148,),
+    (112, 116,),
+    (120, 214, 124, 159, 160, 163, 164, 167, 171, 209, 135, 139,),
     (),
-    (173, 190, 191, 193, 202, 204, 207,),
+    (145, 149, 211, 217, 225, 168, 172,),
+    (113, 117, 126, 130, 161, 165,),
+    (213, 221, 229, 121, 125, 169, 173, 137, 141,),
+    (127, 131, 146, 150, 152, 156, 184, 188,),
+    (215, 216, 220, 224, 228, 128, 132, 138, 151, 162, 166, 175, 179, 185, 189, 192, 196,),
+    (142,),
+    (155, 170, 180, 218, 222, 174, 176, 193, 197,),
+    (226, 230, 129, 133, 449,),
+    (153, 177, 181, 186, 190, 451,),
+    (351, 355, 219, 223, 232, 236, 359, 363, 352, 198, 356, 360, 364,),
+    (227, 231, 233, 237, 194, 453, 377, 381, 384, 388,),
+    (157, 178, 182, 385, 389,),
+    (238, 154, 187, 191, 200, 204, 353, 234, 357,),
+    (183, 361, 365, 400, 401, 404, 405, 408, 412, 376, 380, 450, 455, 199, 201, 195, 158, 205, 386, 390,
+     409, 413, 239, 235, 452, 458, 466, 134, 206, 354, 358, 202, 367, 371, 402, 406, 362, 366, 368, 454,
+     462, 470, 372, 378, 382, 425, 429, 426, 430, 410, 414, 387, 391, 207, 369, 373, 203, 393, 397, 456,
+     457, 461, 465, 469, 379, 383, 392, 403, 396, 407, 416, 420, 433, 437, 240, 427, 431, 459, 463, 434,
+     438, 467, 471, 411, 421, 415, 417, 370, 374, 375, 418, 422, 482, 460, 464, 473, 477, 394, 398, 567,
+     569, 572, 574, 483, 490, 492, 525, 527, 529, 532, 534, 468, 472, 428, 432, 441, 445, 474, 478, 435,
+     439, 419, 423, 424, 573, 575, 395, 399, 475, 479, 491, 493, 485, 487, 484, 510, 512, 568, 570, 577,
+     579, 505, 507, 528, 530, 526, 547, 537, 549, 539, 576, 494, 511, 513, 436, 443, 446, 440, 442, 447,
+     476, 480, 552, 554, 578, 580, 571, 582, 584, 587, 531, 542, 544, 548, 550, 486, 488, 495, 497, 514,
+     506, 508, 557, 515, 559, 517, 444, 448, 481, 581, 583, 588, 585, 538, 540, 551, 589, 543, 489, 500,
+     502, 545, 496, 509, 520, 522, 498, 553, 555, 723, 586, 590, 516, 518, 562, 564, 808, 810, 813, 815,
+     731, 733, 768, 770, 773, 775, 726, 728, 724, 766, 501, 503, 541, 499, 521, 523, 546, 558, 560, 556,
+     519, 814, 816, 533, 535, 732, 734, 563, 565, 809, 811, 818, 820, 769, 771, 778, 780, 504, 774, 524,
+     776, 817, 727, 735, 729, 736, 738, 561, 725, 746, 748, 751, 753, 819, 821, 536, 772, 783, 785, 566,
+     591,),
+    (812, 823, 825, 828, 737, 739, 767, 788, 790, 793, 795,),
+    (752, 754,),
+    (822, 777, 730, 741, 743, 779, 781,),
+    (824, 826, 829, 830, 740, 747, 749, 756, 758,),
+    (755, 784, 786, 789, 791, 798, 800,),
+    (827, 831, 742, 744, 794, 796,),
+    (750, 757, 759, 761, 763, 782,),
+    (787, 792, 803, 805,),
+    (745, 690, 692, 694,),
+    (799, 760, 801,),
+    (592, 596, 762, 764, 797, 696, 600, 604, 593, 597, 601, 605, 618, 622, 625, 626, 629, 630, 617, 621,),
+    (804, 806,),
     (),
-    (160, 162,),
-    (208,),
-    (205,),
-    (163,),
-    (192, 194, 209,),
-    (60, 61, 64, 65, 77, 78, 81, 82,),
+    (765, 802, 594, 598,),
+    (602, 606, 641, 807, 832, 642, 645, 646, 649, 650, 653, 654, 666, 667, 670, 671, 674, 675, 678, 679,),
     (),
+    (627, 631, 691,),
+    (595, 599, 608, 612, 619, 623, 643, 647,),
+    (651, 693, 655, 699, 707, 603, 607, 609, 613,),
+    (620, 624, 628, 632, 633, 634, 637, 638,),
+    (695, 703, 711, 668, 672,),
     (),
-    (195, 62, 66,),
-    (110, 114, 93, 94, 97, 98,),
+    (697, 698, 702, 706, 710, 676, 680,),
+    (931,),
     (),
-    (79, 83, 128, 210, 132, 111, 115,),
-    (126,),
-    (112, 116, 63, 67,),
-    (68, 69, 72, 73, 80, 84, 95, 99, 130,),
-    (),
-    (129, 135, 86, 90, 85, 89,),
-    (),
-    (133, 134, 138,),
-    (),
-    (70, 74, 113, 117, 118, 119, 122, 123, 211, 212, 215, 216,),
-    (127, 136, 232,),
-    (87, 91, 96, 71, 75, 76, 100, 101, 102, 105, 106, 120, 124,),
-    (131, 139, 140, 228,),
-    (261, 265, 88, 92, 229, 244, 248,),
-    (),
-    (107, 103, 234, 279, 245, 249, 213, 283, 125, 121, 233, 262, 266, 230, 137, 147, 142, 217, 277, 141,
-     143, 146, 104, 108, 109, 263, 267, 214, 235, 280, 286, 219, 224, 231, 246, 250, 281, 218, 144, 148,
-     284, 285, 289, 220, 223, 237, 241, 236, 240, 264, 268, 269, 270, 273, 221, 274, 278, 287, 247, 251,
-     252, 253, 256, 257, 271, 145, 149, 150, 275, 225, 238, 242, 222, 258, 282, 254, 226, 227, 290, 291,
-     239, 243, 276, 272, 302, 303, 305, 307, 325, 327, 329, 347, 349, 255, 259, 260, 288, 298, 293, 306,
-     308, 292, 294, 297, 328, 348, 350, 304, 315, 317, 330, 295, 326, 337, 309, 339, 310, 312, 299, 351,
-     352, 354, 357, 331, 332, 334, 316, 318, 296, 300, 301, 338, 340, 311, 313, 453, 454, 333, 335, 456,
-     458, 476, 319, 320, 322, 498, 500, 478, 480, 353, 358, 355, 359, 341, 342, 344, 314, 455, 336, 477,
-     488, 490, 321, 457, 323, 459, 466, 468, 499, 501, 479, 481, 356, 360, 489, 491, 343, 345, 460, 461,
-     463, 324, 467, 469, 482, 483, 485, 502, 503, 505, 508, 492, 346, 493, 495, 470, 471, 473, 361,),
-    (462, 464,),
-    (),
-    (504, 506, 509, 484, 486,),
-    (510,),
-    (472, 474,),
-    (465,),
-    (494, 496,),
-    (507, 511,),
-    (475, 487, 362, 366,),
-    (363, 367,),
-    (497,),
-    (379, 383,),
-    (412, 416, 380, 384,),
-    (),
-    (430, 395, 381, 385, 512, 399,),
-    (364, 368,),
-    (434, 414, 418,),
-    (382, 386,),
-    (365, 369, 370, 371, 374, 375,),
-    (396, 400, 428, 431, 437,),
-    (),
-    (372, 376, 397, 401, 432, 435, 436, 440,),
-    (),
-    (373, 377, 413, 417, 513, 514, 517, 518, 530, 534,),
-    (378, 429, 531, 535,),
-    (398, 402, 388, 392, 387, 391,),
-    (515, 519,),
-    (563, 567, 415, 419, 433, 546, 550,),
-    (532, 536, 547, 551,),
-    (581, 403, 407, 585, 404, 408, 564, 568, 516, 520, 420, 424, 421, 425, 438, 441, 533, 537, 565, 569,
-     579, 405, 409, 422, 426, 442, 521, 525, 522, 526, 548, 552, 583, 439, 582, 588, 406, 410, 423, 427,
-     539, 543, 538, 542, 443, 586, 587, 591, 566, 570, 571, 572, 575, 523, 527, 576, 445, 449, 389, 393,
-     411, 580, 444, 448, 589, 549, 553, 554, 555, 558, 559, 573, 577, 540, 544, 524, 528, 529, 390, 394,
-     446, 450, 584, 592, 593, 560, 541, 545, 556, 578, 447, 451, 452, 574, 590, 600, 595, 557, 594, 596,
-     599, 561, 562, 597, 601, 598, 602, 603,),
+    (833, 837, 700, 704, 610, 614, 644, 648, 657, 661,),
+    (708, 712, 933,),
+    (652, 662, 656, 658, 635,),
+    (701, 705, 714, 718, 639, 669, 673, 659, 663, 682, 686, 935,),
+    (709, 713, 715, 719, 841, 845, 882, 886, 932, 677, 687, 883, 887, 681, 683, 611, 615, 616, 636, 890,
+     894, 720, 834, 716, 838, 640, 660, 664, 665, 835, 839, 842, 846, 684, 688, 934, 937, 884, 888, 940,
+     847, 948, 891, 895, 836, 840, 863, 843, 870, 936, 859, 944, 717, 721, 892, 896, 685, 689, 952, 866,
+     885, 889, 722, 867, 848, 871, 849, 853, 898, 902, 850, 911, 844, 907, 858, 872, 854, 908, 912, 938,
+     939, 947, 943, 915, 919, 951, 893, 897, 899, 903, 868, 904, 851, 855, 909, 913, 941, 873, 862, 860,
+     945, 875, 920, 900, 916, 949, 953, 852, 856, 921, 869, 857, 905, 917, 942, 864, 910, 914, 923, 927,
+     861, 946, 901, 906, 959, 954, 955, 879, 950, 956, 960, 874, 865, 878, 922, 924, 929, 918, 961, 925,
+     928, 957, 876, 880, 962, 930, 958, 926, 877, 881, 963,),
 )
 
 
@@ -170,8 +184,8 @@
 
     def span(color, tags=False):
         start, size = COLS[color]
-        if tags and color == "C":
-            size += EXTRA
+        if tags:
+            start, size = (start, size + EXTRA) if color == TAGGED else (start + EXTRA, size)
         cut = size // 2 // LANE * LANE
         return pl.ds(start, size), (pl.ds(start, cut), pl.ds(start + cut, size - cut))
 
@@ -186,7 +200,7 @@
         value = source(s, h)
         mean = jnp.mean(value * value, -1, keepdims=True)
         normed = (value * lax.rsqrt(mean + epsilon) * gain_ref[...]).astype(jnp.bfloat16)
-        rows[h, 0, 0, 0, :, pl.ds(0, width)] = normed
+        rows[h, 0, 0, 0, :, pl.ds(EXTRA, width)] = normed
         precise = normed.astype(jnp.float32)
         lane = lax.broadcasted_iota(jnp.int32, (BLOCK, EXTRA), 1)
         first_choice = chosen_ref[s, here, 0:1]
@@ -201,7 +215,7 @@
         tags = jnp.where(lane == first_choice, first, 0.0) + jnp.where(
             lane == second_choice, second, 0.0
         )
-        rows[h, 0, 0, 0, :, pl.ds(width, EXTRA)] = tags.astype(jnp.bfloat16)
+        rows[h, 0, 0, 0, :, pl.ds(0, EXTRA)] = tags.astype(jnp.bfloat16)
 
     events = {}
 
@@ -255,14 +269,27 @@
             event(s, h, (color + "y", "e", 0), [crossed], [(color + "y", "n", 0)], lambda: None)
             for y in (0, 1):
                 mid = (lambda p, y=y: (OWN, y, p)) if color == "A" else (lambda p, y=y: (p, y, OWN))
-                last = (lambda p, y=y: (p, y, ALL)) if color == "A" else (lambda p, y=y: (ALL, y, p))
-                end = ring(f"{color}m{y}", color, to_mid, mid, [(color + "y", "e", 0) if y else ready])
-                ends.append(ring(f"{color}l{y}", color, to_last, last, [end]))
+                begun = (color + "y", "e", 0) if y else ready
+                tag = f"{color}m{y}"
+                end = ring(tag, color, to_mid, mid, [begun])
+                near_in = [(tag, "f", 0), (tag, "f", 1)]
+                for (name, piece), need in zip(GATHER_PIECES, ([begun], near_in, [end],)):
+                    last = (
+                        (lambda p, y=y, piece=piece: (p, y, piece))
+                        if color == "A"
+                        else (lambda p, y=y, piece=piece: (piece, y, p))
+                    )
+                    ends.append(ring(f"{color}l{y}{name}", color, to_last, last, need))
         end_x = ring("Cx", "C", to_x, lambda p: (OWN, 0, p), [ready])
-        end_z = ring("Cz", "C", to_z, lambda p: (p, 0, ALL), [end_x])
-        for place, need in ((OWN, end_x), (MINUS, ("Cz", "f", 0)), (PLUS, ("Cz", "f", 1)), (FAR, end_z)):
-            finals.append(across(f"Cy{place}", "C", place, ALL, [need]))
-        event(s, h, ("gathered", "e", 0), finals, ends + [end_z] + [(f"Cy{p}", "n", 0) for p in range(4)],
+        near_in = [("Cx", "f", 0), ("Cx", "f", 1)]
+        ends_z = [
+            ring("Cz" + name, "C", to_z, lambda p, piece=piece: (p, 0, piece), need)
+            for (name, piece), need in zip(GATHER_PIECES, ([ready], near_in, [end_x],))
+        ]
+        came = [[("Cz" + name, "f", way) for name, _ in GATHER_PIECES] for way in (0, 1)]
+        for place, need in ((OWN, [end_x] + near_in), (MINUS, came[0]), (PLUS, came[1]), (FAR, ends_z)):
+            finals.append(across(f"Cy{place}", "C", place, ALL, need))
+        event(s, h, ("gathered", "e", 0), finals, ends + ends_z + [(f"Cy{p}", "n", 0) for p in range(4)],
               lambda: None)
 
     def reduce(s, h):
@@ -271,7 +298,7 @@
         def key(tag, way=0, kind=0):
             return (s, h, "r", tag, way, kind)
 
-        def ring(tag, color, to, place, landing, needs):
+        def ring(tag, color, to, place, landing, far, near, own):
             sides = span(color)[1]
 
             def go(way, kind):
@@ -281,8 +308,8 @@
                      lambda: landing(way, kind), to[way])
 
             for way in (0, 1):
-                event(s, h, (tag, "s", way), [], needs[way], lambda way=way: go(way, 1))
-                event(s, h, (tag, "d", way), [], needs[1 - way], lambda way=way: go(way, 0))
+                event(s, h, (tag, "s", way), [], far(way), lambda way=way: go(way, 1))
+                event(s, h, (tag, "d", way), [], near(way, 1 - way), lambda way=way: go(way, 0))
 
                 def onward(way=way):
                     here = summed(h, *place(GOES[way]), sides[way])()
@@ -290,7 +317,7 @@
                     here[...] = total.astype(jnp.bfloat16)
                     go(way, 2)
 
-                event(s, h, (tag, "p", way), [key(tag, way, 1)], [(tag, "s", way)] + needs[way], onward)
+                event(s, h, (tag, "p", way), [key(tag, way, 1)], [(tag, "s", way)] + near(way, way), onward)
 
                 def finish(way=way):
                     here = summed(h, *place(OWN), sides[way])()
@@ -302,8 +329,15 @@
                     here[...] = total.astype(jnp.bfloat16)
 
                 event(s, h, (tag, "t", way), [key(tag, 1 - way, 0), key(tag, way, 2)],
-                      [(tag, "d", 1 - way), (tag, "p", way)], finish)
-            return [[(tag, "t", 0)], [(tag, "t", 1)]]
+                      [(tag, "d", 1 - way), (tag, "p", way)] + own(way), finish)
+            return [(tag, "t", 0), (tag, "t", 1)]
+
+        def after(tag):
+            return (
+                lambda side: [(tag + "f", "t", side)],
+                lambda way, side: [(tag + "n", "t", side)],
+                lambda side: [(tag + "n", "t", side)],
+            )
 
         def half_cols(color):
             start, size = COLS[color]
@@ -316,25 +350,32 @@
             tile = [("tile", color, 0)]
             for y in (1, 0):
                 mid = (lambda p, y=y: (OWN, y, p)) if color == "A" else (lambda p, y=y: (p, y, OWN))
-                last = (lambda p, y=y: (p, y, ALL)) if color == "A" else (lambda p, y=y: (ALL, y, p))
-                ends = ring(
-                    f"{color}L{y}", color, to_last, last,
-                    lambda way, kind, y=y, color=color: land_last.at[h, y, way, kind, :, :, half_cols(color)],
-                    [tile, tile],
-                )
+                for name, piece in REDUCE_PIECES[::-1]:
+                    last = (
+                        (lambda p, y=y, piece=piece: (p, y, piece))
+                        if color == "A"
+                        else (lambda p, y=y, piece=piece: (piece, y, p))
+                    )
+                    ring(
+                        f"{color}L{y}{name}", color, to_last, last,
+                        lambda way, kind, y=y, color=color, piece=piece: land_last.at[
+                            h, y, way, kind, piece, :, half_cols(color)
+                        ],
+                        lambda side: tile, lambda way, side: tile, lambda side: tile,
+                    )
                 ends = ring(
                     f"{color}M{y}", color, to_mid, mid,
                     lambda way, kind, y=y, color=color: land_mid.at[h, y, way, kind, :, half_cols(color)],
-                    ends,
+                    *after(f"{color}L{y}"),
                 )
                 if y == 1:
-                    event(s, h, (color + "Y", "n", 0), [], ends[0] + ends[1], lambda color=color, cols=cols: send(
+                    event(s, h, (color + "Y", "n", 0), [], ends, lambda color=color, cols=cols: send(
                         key(color + "Y"), group, summed(h, OWN, 1, OWN, cols),
                         lambda: land_y.at[h, 0, 0, :, cols], partner))
                     finals.append((color + "Y", "n", 0))
                     arrivals.append(key(color + "Y"))
                 else:
-                    finals += ends[0] + ends[1]
+                    finals += ends
         c_cols = span("C")[0]
         for z in range(4):
             event(s, h, (f"CY{z}", "n", 0), [], [("tile", "C", 0)], lambda z=z: send(
@@ -347,27 +388,27 @@
                 here[...] = total.astype(jnp.bfloat16)
 
             event(s, h, (f"CY{z}", "a", 0), [key("CY", z)], [(f"CY{z}", "n", 0)], add)
-        all_z = [(f"CY{z}", "a", 0) for z in range(4)]
-        ends = ring("CZ", "C", to_z, lambda p: (p, 0, ALL),
-                    lambda way, kind: land_last.at[h, 0, way, kind, :, :, half_cols("C")], [all_z, all_z])
-        for way in (0, 1):
-            near = (f"CY{GOES[way]}", "a", 0)
-            events[s, h, ("CZ", "s", way)].needs[:] = [(f"CY{FAR}", "a", 0)]
-            events[s, h, ("CZ", "d", way)].needs[:] = [near]
-            events[s, h, ("CZ", "p", way)].needs[:] = [("CZ", "s", way), near]
-            events[s, h, ("CZ", "t", way)].needs.append((f"CY{OWN}", "a", 0))
+        for name, piece in REDUCE_PIECES[::-1]:
+            ring(
+                "CZ" + name, "C", to_z, lambda p, piece=piece: (p, 0, piece),
+                lambda way, kind, piece=piece: land_last.at[h, 0, way, kind, piece, :, half_cols("C")],
+                lambda side: [(f"CY{FAR}", "a", 0)],
+                lambda way, side: [(f"CY{GOES[way]}", "a", 0)],
+                lambda side: [(f"CY{OWN}", "a", 0)],
+            )
         ends = ring("CX", "C", to_x, lambda p: (OWN, 0, p),
-                    lambda way, kind: land_mid.at[h, 0, way, kind, :, half_cols("C")], ends)
-        finals += ends[0] + ends[1]
+                    lambda way, kind: land_mid.at[h, 0, way, kind, :, half_cols("C")], *after("CZ"))
+        finals += ends
 
         def total_of():
             here = pl.ds(h * BLOCK, BLOCK)
             total = source(s, h) + part[h, 0, 0, 0, :, :].astype(jnp.float32)
-            ab = pl.ds(0, COLS["C"][0])
-            mine[s, here, ab] = (
-                total[:, : COLS["C"][0]] + land_y[h, 0, 0, :, ab].astype(jnp.float32)
-            ).astype(jnp.bfloat16)
-            mine[s, here, c_cols] = total[:, COLS["C"][0] :].astype(jnp.bfloat16)
+            for color in "ABC":
+                start, size = COLS[color]
+                value = total[:, start : start + size]
+                if color != "C":
+                    value = value + land_y[h, 0, 0, :, start : start + size].astype(jnp.float32)
+                mine[s, here, start : start + size] = value.astype(jnp.bfloat16)
             send((s, h, "r", "relay", 0), "relay", lambda: mine.at[s, here, :],
                  lambda: relay.at[s, here, :], following)
 
@@ -377,7 +418,7 @@
 
     def hidden_tile(h, j):
         both = jnp.dot(
-            rows[h, :, :, :, :, pl.ds(0, width)].reshape(512, width), wide[j],
+            rows[h, :, :, :, :, pl.ds(EXTRA, width)].reshape(512, width), wide[j],
             preferred_element_type=jnp.float32,
         )
         gate = both[:, :LANE]
@@ -385,7 +426,7 @@
         hidden[:, pl.ds(pl.multiple_of(j * LANE, LANE), LANE)] = value.astype(jnp.bfloat16)
 
     def start_part(s, h):
-        tags = rows[h, :, :, :, :, pl.ds(width, EXTRA)].reshape(512, EXTRA).astype(jnp.float32)
+        tags = rows[h, :, :, :, :, pl.ds(0, EXTRA)].reshape(512, EXTRA).astype(jnp.float32)
         share[...] = jnp.sum(jnp.where(lanes == cx, tags, 0.0), 1, keepdims=True)
         drain(("g", s, h))
         drain(("r", s - 1, h))
@@ -425,12 +466,11 @@
     names = list(events)
     slots = iter(SCHEDULE)
 
-    def now():
-        for n in next(slots):
-            events[names[n]].run()
-
+    first, *others = next(slots)
+    events[names[first]].run()
     wait(barrier, 7)
-    now()
+    for n in others:
+        events[names[n]].run()
     for copy in loads:
         copy.wait()
     for s in range(STEPS):
@@ -464,7 +504,7 @@
     tokens, width = pending.shape
     ff = gate_cols.shape[1]
     bf16 = jnp.bfloat16
-    copies = 2 * (2 * 17 + 12 + 2 * 25 + 16 + 2)
+    copies = 368
     return pl.pallas_call(
         kernel,
         out_shape=jax.ShapeDtypeStruct((STEPS, tokens, width), bf16),

time: 208 us -> 200 us (0.962)
  Pallas kernels: 204 us -> 196 us
    pallas_call x1, Pallas kernels: 204 us -> 196 us  [both_steps(): pl.pallas_call(kernel, out_shape=jax.ShapeDtypeStruct((STEPS, tokens, wid...]
where the time goes in v4:
time: 200 us
  Pallas kernels  196 us (98%)
  local copies, waits for them, and re-layouts  3.25 us (2%)
    pallas_call x1, Pallas kernels, both_steps(): pl.pallas_call(kernel, out_shape=jax.ShapeDtypeStruct((STEPS, tokens, wid...  196 us

profile of v4, /device:TPU:1, one launch (start us, length us, event | category | flops | bytes accessed | tf_op | source)
XLA Modules:
  0.0 199.7 jit_solution(17011599714532175720)
XLA Ops:
  0.0 1.4 copy.9.chosen_ref
  1.4 196.5 %both_steps.1 = bf16[2,32,4096]{2,1,0:T(8,128)(2,1)} custom-call(bf16[32,4096]{1,0:T(8,128)(2,1)} %bitcast.16, bf16[32,4096]{1,0:T(8,128)(2,1)} %bitcast.17, s32[2,32,2]{2,1,0:T(8,128)} %copy.9.chosen_ref, f32[1,4096]{1,0:T(1,128)} %gain_ref.1, f32[4,4096]{1,0:T(4,128)} %bitcast.18, bf16[4096,896]{1,0:T(8,128)(2,1)} %bitcast.12, bf16[4096,896]{1,0:T(8,128)(2,1)} %bitcast.13, ...), custom_call_target="tpu_custom_call" | custom-call | tf_op jit(solution)/shard_map/both_steps/pallas_call | solution.py:508
  197.9 1.9 copy.12

commit v5 on v4

--- a/solution.py
+++ b/solution.py
@@ -10,7 +10,7 @@
 EXTRA = 128
 BLOCK = 16
 LANE = 128
-MESH = pl.DeviceIdType.MESH
+LOGICAL = pl.DeviceIdType.LOGICAL
 
 epsilon = 1e-05
 
@@ -132,13 +132,13 @@
     cx, cy, cz = e // 8, (e // 4) % 2, e % 4
 
     def at(x, y, z):
-        return {"section": section, "expert": x * 8 + y * 4 + z}
+        return section * 32 + x * 8 + y * 4 + z
 
     to_x = (at(lax.rem(cx + 1, 4), cy, cz), at(lax.rem(cx + 3, 4), cy, cz))
     to_z = (at(cx, cy, lax.rem(cz + 1, 4)), at(cx, cy, lax.rem(cz + 3, 4)))
     partner = at(cx, 1 - cy, cz)
-    following = {"section": lax.rem(section + 1, 4), "expert": e}
-    preceding = {"section": lax.rem(section + 3, 4), "expert": e}
+    following = lax.rem(section + 1, 4) * 32 + e
+    preceding = lax.rem(section + 3, 4) * 32 + e
 
     loads = []
 
@@ -154,7 +154,7 @@
 
     barrier = pltpu.get_barrier_semaphore()
     for device in (*to_x, *to_z, partner, following, preceding):
-        pl.semaphore_signal(barrier, inc=1, device_id=device, device_id_type=MESH)
+        pl.semaphore_signal(barrier, inc=1, device_id=device, device_id_type=LOGICAL)
 
     numbers = {}
     known = {}
@@ -164,7 +164,7 @@
         n = numbers.setdefault(key if "relay" in key else key[1:], len(numbers))
         known[key] = lambda: pltpu.make_async_remote_copy(
             src_ref=src(), dst_ref=dst(), send_sem=send_sems.at[n], recv_sem=recv_sems.at[n],
-            device_id=device, device_id_type=MESH,
+            device_id=device, device_id_type=LOGICAL,
         )
         known[key]().start()
         flying.setdefault(group, []).append(known[key])

time: 200 us -> 200 us (level)
  no operation moved by 1% of the time
where the time goes in v5:
time: 200 us
  Pallas kernels  196 us (98%)
  local copies, waits for them, and re-layouts  3.25 us (2%)
    pallas_call x1, Pallas kernels, both_steps(): pl.pallas_call(kernel, out_shape=jax.ShapeDtypeStruct((STEPS, tokens, wid...  196 us

profile of v5, /device:TPU:1, one launch (start us, length us, event | category | flops | bytes accessed | tf_op | source)
XLA Modules:
  0.0 199.7 jit_solution(4337693056673095882)
XLA Ops:
  0.0 1.4 copy.9.chosen_ref
  1.4 196.5 %both_steps.1 = bf16[2,32,4096]{2,1,0:T(8,128)(2,1)} custom-call(bf16[32,4096]{1,0:T(8,128)(2,1)} %bitcast.16, bf16[32,4096]{1,0:T(8,128)(2,1)} %bitcast.17, s32[2,32,2]{2,1,0:T(8,128)} %copy.9.chosen_ref, f32[1,4096]{1,0:T(1,128)} %gain_ref.1, f32[4,4096]{1,0:T(4,128)} %bitcast.18, bf16[4096,896]{1,0:T(8,128)(2,1)} %bitcast.12, bf16[4096,896]{1,0:T(8,128)(2,1)} %bitcast.13, ...), custom_call_target="tpu_custom_call" | custom-call | tf_op jit(solution)/shard_map/both_steps/pallas_call | solution.py:508
  197.9 1.9 copy.12
